TPU v7x, 8 devices: a whole 2x2x1 slice. The times are simulated.
8 devices in a mesh: dp: 2 (over z, y), ep: 4 (over x, core).
Axes of the slice: x: 2, y: 2, z: 1, core: 2. Of those that a mesh axis runs over, the one named last changes fastest.
Arguments:
- x_in: bfloat16 [4096, 512], P(('dp', 'ep')), parts along dimension 0
- idx_a: int32 [4096, 2], P(('dp', 'ep')), parts along dimension 0
- idx_b: int32 [4096, 2], P(('dp', 'ep')), parts along dimension 0
- gate_a: float32 [4096, 2], P(('dp', 'ep')), parts along dimension 0
- gate_b: float32 [4096, 2], P(('dp', 'ep')), parts along dimension 0
- dy_out: bfloat16 [4096, 512], P(('dp', 'ep')), parts along dimension 0
- w1_a: bfloat16 [8, 512, 1792], P('ep')
- w3_a: bfloat16 [8, 512, 1792], P('ep')
- w2_a: bfloat16 [8, 1792, 512], P('ep')
- w1_b: bfloat16 [8, 512, 1792], P('ep')
- w3_b: bfloat16 [8, 512, 1792], P('ep')
- w2_b: bfloat16 [8, 1792, 512], P('ep')
Outputs:
- output 1: bfloat16 [4096, 512], P(('dp', 'ep')), parts along dimension 0
- output 2: bfloat16 [4096, 512], P(('dp', 'ep')), parts along dimension 0
- output 3: float32 [16, 512, 1792], P(('dp', 'ep')), parts along dimension 0
- output 4: float32 [16, 512, 1792], P(('dp', 'ep')), parts along dimension 0
- output 5: float32 [16, 1792, 512], P(('dp', 'ep')), parts along dimension 0
- output 6: float32 [16, 512, 1792], P(('dp', 'ep')), parts along dimension 0
- output 7: float32 [16, 512, 1792], P(('dp', 'ep')), parts along dimension 0
- output 8: float32 [16, 1792, 512], P(('dp', 'ep')), parts along dimension 0
- output 9: float32 [4096, 2], P(('dp', 'ep')), parts along dimension 0
- output 10: float32 [4096, 2], P(('dp', 'ep')), parts along dimension 0
There are 2 independent parts. A program takes and returns all parts, laid end to end along the dimension named above; an argument that names none is the same for every part.
All inputs are finite; a program needn't handle non-finite values.
Results may differ from a plain program's by a relative error of at most 0.00787.
Values are sent between devices in bfloat16 or wider.
A program may use at most 1 GiB of HBM per device.

v0:
```python
import functools

import jax
import jax.numpy as jnp
from jax import lax
from jax.experimental import pallas as pl
from jax.experimental.pallas import tpu as pltpu
from jax.sharding import PartitionSpec as P


ROWS = 256
TOKS = 256
ALIGN = 16
COLS = 256
EXPERTS = 2
VMEM = 66_000_000

BF = jnp.bfloat16
F32 = jnp.float32


def mm(a, b):
    return lax.dot_general(a, b, (((1,), (0,)), ((), ())), preferred_element_type=F32)


def mm_nt(a, b):
    return lax.dot_general(a, b, (((1,), (1,)), ((), ())), preferred_element_type=F32)


def mm_tn(a, b):
    return lax.dot_general(a, b, (((0,), (0,)), ((), ())), preferred_element_type=F32)


def block_of(refs, b):
    per = refs[0].shape[0] // TOKS
    return refs[b // per], slice((b % per) * TOKS, (b % per + 1) * TOKS)


def tile_rows(k):
    return pl.ds(pl.multiple_of(k * ROWS, ROWS), ROWS)


class Slots:
    def __init__(self, starts_ref, rows_ref, cols_ref, blocks):
        self.starts_ref, self.rows_ref, self.cols_ref, self.blocks = starts_ref, rows_ref, cols_ref, blocks

    def tiles(self, e):
        return (self.starts_ref[e, self.blocks] + ROWS - 1) // ROWS

    def rows(self, e, b):
        return pl.ds(pl.multiple_of(self.starts_ref[e, b], ALIGN), TOKS)

    def base(self, e, b):
        return self.starts_ref[e, b].astype(F32)

    def col(self, b, i):
        rows = slice(b * TOKS, (b + 1) * TOKS) if isinstance(b, int) else pl.ds(pl.multiple_of(b * TOKS, TOKS), TOKS)
        return self.cols_ref[rows, i : i + 1]

    def gate(self, e, b):
        if isinstance(e, int):
            return self.col(b, EXPERTS + e)
        return jnp.where(e == 0, self.col(b, EXPERTS), self.col(b, EXPERTS + 1))

    def choice(self, e, b):
        return self.col(b, 2 * EXPERTS + e)

    def compact(self, e, makers, outs):
        line = lax.broadcasted_iota(jnp.int32, (TOKS, TOKS), 0).astype(F32)
        for b in range(self.blocks):
            slot = self.rows_ref[pl.ds(e, 1), b * TOKS : (b + 1) * TOKS] - self.base(e, b)
            hot = jnp.where(slot == line, 1.0, 0.0).astype(BF)
            for make, out in zip(makers, outs):
                out[self.rows(e, b), :] = mm(hot, make(b)).astype(BF)
        end = pl.multiple_of(self.starts_ref[e, self.blocks - 1] + TOKS, ALIGN)
        for out in outs:
            out[pl.ds(end, ROWS), :] = jnp.zeros((ROWS, out.shape[1]), BF)

    def spread(self, e, b, ref, more=0):
        line = lax.broadcasted_iota(jnp.int32, (TOKS, TOKS + more), 1).astype(F32)
        hot = jnp.where(self.col(b, e) - self.base(e, b) == line, 1.0, 0.0).astype(BF)
        rows = pl.ds(pl.multiple_of(self.starts_ref[e, b], ALIGN), TOKS + more)
        return mm(hot, ref[rows, :])

    def zero_after(self, e, ref):
        end = pl.multiple_of(self.tiles(e) * ROWS, ROWS)
        ref[pl.ds(end, TOKS + ALIGN), :] = jnp.zeros((TOKS + ALIGN, ref.shape[1]), BF)


def find_slots(tables, refs):
    full_a, full_b, halves = refs[0:3], refs[3:6], (refs[6:9], refs[9:12])
    tok = tables[0].shape[1]
    blocks = len(tables) * tok // TOKS
    half = blocks // 2
    first = (lax.axis_index("ep") * EXPERTS).astype(F32)
    line = lax.broadcasted_iota(jnp.int32, (8, TOKS), 0)
    target = first + (line % EXPERTS).astype(F32)
    lane = lax.broadcasted_iota(jnp.int32, (8, 128), 1)
    upto = (lax.broadcasted_iota(jnp.int32, (TOKS, TOKS), 0) <= lax.broadcasted_iota(jnp.int32, (TOKS, TOKS), 1)).astype(F32).astype(BF)
    seen = jnp.zeros((8, 1), F32)
    before = jnp.zeros((8, 1), F32)
    starts = jnp.zeros((8, 128), F32)
    later = jnp.zeros((8, 128), F32)
    for b in range(blocks):
        at = b * TOKS
        table = tables[at // tok][:, at % tok : at % tok + TOKS]
        if b == half:
            before = seen

        def both(i, other):
            return jnp.where(line < EXPERTS, table[i : i + 1], jnp.where(line < 2 * EXPERTS, table[i + 2 : i + 3], other))

        hit0 = both(0, -1.0) == target
        hit1 = both(1, -1.0) == target
        mask = jnp.where(hit0 | hit1, 1.0, 0.0)
        count = mm(mask.astype(BF), upto)
        slot = jnp.where(mask > 0.0, seen + count - 1.0, -1.0)
        part_slot = jnp.where(mask > 0.0, seen - before + count - 1.0, -1.0)
        gate = jnp.where(hit0, both(4, 0.0), 0.0) + jnp.where(hit1, both(5, 0.0), 0.0)
        choice = jnp.where(hit1, 1.0, 0.0)
        starts = jnp.where(lane == b, seen, starts)
        if b >= half:
            later = jnp.where(lane == b - half, seen - before, later)

        def put(outs, layer, here, slots):
            part = slice(layer * EXPERTS, (layer + 1) * EXPERTS)
            outs[1][:, here : here + TOKS] = slots[part]
            stack = jnp.concatenate([slots[part], gate[part], choice[part], choice[part]], axis=0)
            outs[2][here : here + TOKS, :] = stack.T

        put(full_a, 0, at, slot)
        put(full_b, 1, at, slot)
        put(halves[b // half], 0, at % (half * TOKS), part_slot)
        seen = seen + jnp.floor((count[:, TOKS - 1 :] + (ALIGN - 1.0)) / ALIGN) * ALIGN
    starts = jnp.where(lane == blocks, seen, starts).astype(jnp.int32)
    later = jnp.where(lane == half, seen - before, later).astype(jnp.int32)
    full_a[0][...] = starts[:EXPERTS]
    full_b[0][...] = starts[EXPERTS : 2 * EXPERTS]
    halves[0][0][...] = starts[:EXPERTS]
    halves[1][0][...] = later[:EXPERTS]


def gather_kernel(map_ref, x_ref, other_hbm, diagonal_hbm, mate_hbm, *refs):
    slot_hbm, slot_refs = refs[:12], refs[12:24]
    maps, held, map_send, map_recv, far_send, far_recv, hop_send, hop_recv, near_send, near_recv, out_sems, slot_sems = refs[24:]
    me = lax.axis_index("ep")
    mate = me + 1 - 2 * lax.rem(me, 2)
    other = lax.rem(me + 2, 4)
    diagonal = lax.rem(mate + 2, 4)
    pieces = far_send.shape[0]
    size = x_ref.shape[0] // pieces

    def send(src, dst, send_sem, recv_sem, to):
        return pltpu.make_async_remote_copy(
            src_ref=src, dst_ref=dst, send_sem=send_sem, recv_sem=recv_sem,
            device_id={"ep": to}, device_id_type=pl.DeviceIdType.MESH,
        )

    barrier = pltpu.get_barrier_semaphore()
    for peer in (other, diagonal, mate):
        pl.semaphore_signal(barrier, inc=1, device_id={"ep": peer}, device_id_type=pl.DeviceIdType.MESH)
    pl.semaphore_wait(barrier, 3)

    map_copies = [send(map_ref, maps.at[i], map_send.at[i], map_recv.at[i], to) for i, to in enumerate((other, diagonal, mate))]
    for copy in map_copies:
        copy.start()
    part = [pl.ds(p * size, size) for p in range(pieces)]
    far = [send(x_ref.at[part[p], :], held.at[0, part[p], :], far_send.at[p], far_recv.at[p], other) for p in range(pieces)]
    for copy in far:
        copy.start()
    near = send(x_ref, held.at[2], near_send, near_recv, mate)
    near.start()
    for copy in map_copies:
        copy.wait_recv()
    find_slots((maps.at[0], maps.at[1], map_ref, maps.at[2]), slot_refs)
    slot_copies = [pltpu.make_async_copy(v, h, slot_sems.at[i]) for i, (v, h) in enumerate(zip(slot_refs, slot_hbm))]
    for copy in slot_copies:
        copy.start()
    near.wait()
    outs = [pltpu.make_async_copy(held.at[2], mate_hbm, out_sems.at[2 * pieces])]
    outs[0].start()
    hops = []
    for p in range(pieces):
        far[p].wait_recv()
        hops.append(send(held.at[0, part[p], :], held.at[1, part[p], :], hop_send.at[p], hop_recv.at[p], mate))
        hops[p].start()
        outs.append(pltpu.make_async_copy(held.at[0, part[p], :], other_hbm.at[part[p], :], out_sems.at[p]))
        outs[-1].start()
    for p in range(pieces):
        hops[p].wait_recv()
        outs.append(pltpu.make_async_copy(held.at[1, part[p], :], diagonal_hbm.at[part[p], :], out_sems.at[pieces + p]))
        outs[-1].start()
    for copy in map_copies + far + hops:
        copy.wait_send()
    for copy in outs + slot_copies:
        copy.wait()


def weight_copies(hbm, vmem, sems, e):
    return [pltpu.make_async_copy(h.at[e], v.at[e], sems.at[e, i]) for i, (h, v) in enumerate(zip(hbm, vmem))]


def forward_kernel(n, starts_ref, *refs):
    xs, (rows_ref, cols_ref, w1_hbm, w3_hbm, w2_hbm), ys = refs[:n], refs[n : n + 5], refs[n + 5 : 2 * n + 5]
    w1, w3, w2, u_all, o_all, h_ref, y_buf, w_sems, y_sems = refs[2 * n + 5 :]
    blocks = rows_ref.shape[1] // TOKS
    width = w1.shape[2]
    slots = Slots(starts_ref, rows_ref, cols_ref, blocks)
    for e in range(EXPERTS):
        for copy in weight_copies((w1_hbm, w3_hbm, w2_hbm), (w1, w3, w2), w_sems, e):
            copy.start()

    def tokens_of(b):
        ref, toks = block_of(xs, b)
        return ref[toks, :]

    def gather_rows(e, carry):
        slots.compact(e, (tokens_of,), (u_all.at[e],))
        return carry

    lax.fori_loop(0, EXPERTS, gather_rows, 0)

    def expert(e, carry):
        for copy in weight_copies((w1_hbm, w3_hbm, w2_hbm), (w1, w3, w2), w_sems, e):
            copy.wait()

        def tile(k, inner):
            u = u_all[e, tile_rows(k), :]
            for c in range(0, width, COLS):
                cols = slice(c, c + COLS)
                a = mm(u, w1[e, :, cols])
                b = mm(u, w3[e, :, cols])
                h_ref[:, cols] = (a * jax.nn.sigmoid(a) * b).astype(BF)
            o_all[e, tile_rows(k), :] = mm(h_ref[...], w2[e]).astype(BF)
            return inner

        return lax.fori_loop(0, slots.tiles(e), tile, carry)

    lax.fori_loop(0, EXPERTS, expert, 0)
    for e in range(EXPERTS):
        slots.zero_after(e, o_all.at[e])
    each = ys[0].shape[0] // TOKS

    def send_home(i, carry):
        for j in range(each):
            b = i * each + j
            toks = slice(j * TOKS, (j + 1) * TOKS)
            y_buf[i, toks, :] = sum(slots.gate(e, b) * slots.spread(e, b, o_all.at[e]) for e in range(EXPERTS))
        for n, ref in enumerate(ys):
            pl.when(i == n)(lambda: pltpu.make_async_copy(y_buf.at[n], ref, y_sems.at[n]).start())
        return carry

    lax.fori_loop(0, len(ys), send_home, 0)
    for n, ref in enumerate(ys):
        pltpu.make_async_copy(y_buf.at[n], ref, y_sems.at[n]).wait()


def dx_kernel(starts_ref, x0, x1, x2, x3, g0, g1, g2, g3, rows_ref, cols_ref, w1_hbm, w3_hbm, w2_hbm,
              dx0, dx1, dx2, dx3, kept_hbm, w1, w3, w2, u_all, q_all, od_all, kept, dx_buf, w_sems, k_sems, dx_sems):
    xs, gs, dxs = (x0, x1, x2, x3), (g0, g1, g2, g3), (dx0, dx1, dx2, dx3)
    tok = x0.shape[0]
    blocks = rows_ref.shape[1] // TOKS
    dim, width = w1.shape[1:]
    slots = Slots(starts_ref, rows_ref, cols_ref, blocks)
    for e in range(EXPERTS):
        for copy in weight_copies((w1_hbm, w3_hbm, w2_hbm), (w1, w3, w2), w_sems, e):
            copy.start()

    def tokens_of(b):
        ref, toks = block_of(xs, b)
        return ref[toks, :]

    def gather_rows(e, carry):
        def scaled_of(b):
            ref, toks = block_of(gs, b)
            return (slots.gate(e, b) * ref[toks, :].astype(F32)).astype(BF)

        slots.compact(e, (tokens_of, scaled_of), (u_all.at[e], q_all.at[e]))
        return carry

    lax.fori_loop(0, EXPERTS, gather_rows, 0)

    def copy_out(e, k):
        return pltpu.make_async_copy(kept.at[lax.rem(k, 2)], kept_hbm.at[e, tile_rows(k), :], k_sems.at[lax.rem(k, 2)])

    def expert(e, carry):
        for copy in weight_copies((w1_hbm, w3_hbm, w2_hbm), (w1, w3, w2), w_sems, e):
            copy.wait()
        count = slots.tiles(e)

        def tile(k, inner):
            slot = lax.rem(k, 2)

            @pl.when(k >= 2)
            def _():
                copy_out(e, k - 2).wait()

            u = u_all[e, tile_rows(k), :]
            q = q_all[e, tile_rows(k), :]
            for c in range(0, width, COLS):
                cols = slice(c, c + COLS)
                a = mm(u, w1[e, :, cols])
                b = mm(u, w3[e, :, cols])
                dh = mm_nt(q, w2[e, cols, :])
                s = jax.nn.sigmoid(a)
                act = a * s
                kept[slot, :, c : c + COLS] = (act * b).astype(BF)
                kept[slot, :, width + c : width + c + COLS] = (dh * b * s * (1.0 + a * (1.0 - s))).astype(BF)
                kept[slot, :, 2 * width + c : 2 * width + c + COLS] = (dh * act).astype(BF)
            kept[slot, :, 3 * width : 3 * width + dim] = u
            kept[slot, :, 3 * width + dim :] = q
            od_all[e, tile_rows(k), :dim] = mm(kept[slot, :, :width], w2[e]).astype(BF)
            du = mm_nt(kept[slot, :, width : 2 * width], w1[e]) + mm_nt(kept[slot, :, 2 * width : 3 * width], w3[e])
            od_all[e, tile_rows(k), dim:] = du.astype(BF)
            copy_out(e, k).start()
            return inner

        lax.fori_loop(0, count, tile, 0)

        @pl.when(count >= 2)
        def _():
            copy_out(e, count - 2).wait()

        @pl.when(count >= 1)
        def _():
            copy_out(e, count - 1).wait()

        return carry

    lax.fori_loop(0, EXPERTS, expert, 0)
    for e in range(EXPERTS):
        slots.zero_after(e, od_all.at[e])
    copies = []
    each = tok // TOKS
    lane = lax.broadcasted_iota(jnp.int32, (TOKS, 8), 1).astype(F32)
    for i, ref in enumerate(dxs):

        for j in range(each):
            b = i * each + j
            toks = slice(j * TOKS, (j + 1) * TOKS)
            dy = gs[i][toks, :].astype(F32)
            dx = jnp.zeros((TOKS, dim), F32)
            dg = jnp.zeros((TOKS, 8), F32)
            for e in range(EXPERTS):
                od = slots.spread(e, b, od_all.at[e], ALIGN)
                dx += od[:, dim:]
                dg += jnp.where(lane == slots.choice(e, b), jnp.sum(dy * od[:, :dim], axis=1, keepdims=True), 0.0)
            dx_buf[i, toks, :] = dx
            dx_buf[i, tok : tok + 8, toks] = dg.T
        copies.append(pltpu.make_async_copy(dx_buf.at[i], ref, dx_sems.at[i]))
        copies[-1].start()
    for copy in copies:
        copy.wait()


def dw_kernel(starts_ref, kept_hbm, dw1_hbm, dw3_hbm, dw2_hbm, kept, dw1, dw3, dw2, k_sems, o_sems):
    dim, width = dw1.shape[1:]
    slots = Slots(starts_ref, None, None, kept_hbm.shape[1] // TOKS)

    def copy_in(e, k, slot):
        rows = pl.ds(pl.multiple_of(k * 2 * ROWS, 2 * ROWS), 2 * ROWS)
        return pltpu.make_async_copy(kept_hbm.at[e, rows, :], kept.at[slot], k_sems.at[slot])

    def copy_out(e, i):
        return pltpu.make_async_copy((dw1, dw3, dw2)[i].at[e], (dw1_hbm, dw3_hbm, dw2_hbm)[i].at[e], o_sems.at[e, i])

    first = (slots.tiles(1) > slots.tiles(0)).astype(jnp.int32)
    first_tiles = (slots.tiles(first) + 1) // 2
    count = first_tiles + (slots.tiles(1 - first) + 1) // 2

    def where(g):
        second = (g >= first_tiles).astype(jnp.int32)
        return jnp.where(second == 0, first, 1 - first), g - second * first_tiles

    copy_in(*where(0), 0).start()

    def tile(g, carry):
        slot = lax.rem(g, 2)
        e, k = where(g)
        copy_in(e, k, slot).wait()

        @pl.when(g + 1 < count)
        def _():
            copy_in(*where(g + 1), 1 - slot).start()

        @pl.when(2 * k + 1 == slots.tiles(e))
        def _():
            kept[slot, ROWS:, :] = jnp.zeros((ROWS, kept.shape[2]), BF)

        u = kept[slot, :, 3 * width : 3 * width + dim]
        q = kept[slot, :, 3 * width + dim :]
        fresh = k == 0
        last = (g == first_tiles - 1) | (g == count - 1)

        def put(ref, index, part):
            ref[index] = jnp.where(fresh, part, ref[index] + part)

        def leave(i):
            pl.when(last)(lambda: copy_out(e, i).start())

        for c in range(0, width, COLS):
            put(dw1, (e, slice(None), slice(c, c + COLS)), mm_tn(u, kept[slot, :, width + c : width + c + COLS]))
        leave(0)
        for c in range(0, width, COLS):
            put(dw3, (e, slice(None), slice(c, c + COLS)), mm_tn(u, kept[slot, :, 2 * width + c : 2 * width + c + COLS]))
        leave(1)
        for c in range(0, width, COLS):
            put(dw2, (e, slice(c, c + COLS), slice(None)), mm_tn(kept[slot, :, c : c + COLS], q))
        leave(2)
        return carry

    lax.fori_loop(0, count, tile, 0)
    for e in range(EXPERTS):
        for i in range(3):
            copy_out(e, i).wait()


IN_VMEM = pl.BlockSpec(memory_space=pltpu.VMEM)
IN_SMEM = pl.BlockSpec(memory_space=pltpu.SMEM)
IN_HBM = pl.BlockSpec(memory_space=pl.ANY)


def call(kernel, operands, in_specs, outs, out_specs, scratch, flops):
    return pl.pallas_call(
        kernel,
        in_specs=in_specs,
        out_specs=out_specs,
        out_shape=outs,
        scratch_shapes=scratch,
        compiler_params=pltpu.CompilerParams(vmem_limit_bytes=VMEM),
        cost_estimate=pl.CostEstimate(flops=flops, bytes_accessed=40_000_000, transcendentals=0),
    )(*operands)


def run_gather(own_map, x):
    tok, dim = x.shape
    tokens = 4 * tok
    pieces = 4
    outs = []
    for size in (tokens, tokens, tokens // 2, tokens // 2):
        outs.append(jax.ShapeDtypeStruct((EXPERTS, 128), jnp.int32))
        outs.append(jax.ShapeDtypeStruct((EXPERTS, size), F32))
        outs.append(jax.ShapeDtypeStruct((size, 8), F32))
    dma = pltpu.SemaphoreType.DMA
    out = pl.pallas_call(
        gather_kernel,
        in_specs=[IN_VMEM] * 2,
        out_specs=[IN_HBM] * 15,
        out_shape=[jax.ShapeDtypeStruct((tok, dim), BF)] * 3 + outs,
        scratch_shapes=[pltpu.VMEM(out.shape, out.dtype) for out in outs]
        + [pltpu.VMEM((3, *own_map.shape), F32), pltpu.VMEM((3, tok, dim), BF)]
        + [dma((3,)), dma((3,))] + [dma((pieces,))] * 4 + [dma, dma, dma((2 * pieces + 1,)), dma((12,))],
        compiler_params=pltpu.CompilerParams(collective_id=0, has_side_effects=True, vmem_limit_bytes=VMEM),
        cost_estimate=pl.CostEstimate(flops=10_000_000, bytes_accessed=4_000_000, transcendentals=0),
        name="gather_slots",
    )(own_map, x)
    maps = out[3:]
    return (out[0], out[1], x, out[2]), (maps[0:3], maps[3:6], maps[6:9], maps[9:12])


def weight_scratch(w1, w2):
    return [pltpu.VMEM(w1.shape, BF), pltpu.VMEM(w1.shape, BF), pltpu.VMEM(w2.shape, BF)]


def run_forward(xs, maps, w1, w3, w2):
    tok, dim = xs[0].shape
    tokens = tok * len(xs)
    width = w1.shape[2]
    most = tokens + TOKS + ALIGN + ROWS
    return call(
        functools.partial(forward_kernel, len(xs)), (maps[0], *xs, maps[1], maps[2], w1, w3, w2),
        [IN_SMEM] + [IN_VMEM] * (len(xs) + 2) + [IN_HBM] * 3,
        [jax.ShapeDtypeStruct((tok, dim), F32)] * len(xs),
        [IN_HBM] * len(xs),
        weight_scratch(w1, w2)
        + [pltpu.VMEM((EXPERTS, most, dim), BF)] * 2
        + [pltpu.VMEM((ROWS, width), BF), pltpu.VMEM((len(xs), tok, dim), F32)]
        + [pltpu.SemaphoreType.DMA((EXPERTS, 3)), pltpu.SemaphoreType.DMA((len(xs),))],
        2 * 3 * tokens * dim * width,
    )


def run_dx(xs, gs, maps, w1, w3, w2):
    tok, dim = xs[0].shape
    tokens = tok * len(xs)
    width = w1.shape[2]
    most = tokens + TOKS + ALIGN + ROWS
    kept = 3 * width + 2 * dim
    out = call(
        dx_kernel, (maps[0], *xs, *gs, maps[1], maps[2], w1, w3, w2),
        [IN_SMEM] + [IN_VMEM] * 10 + [IN_HBM] * 3,
        [jax.ShapeDtypeStruct((tok + 8, dim), F32)] * 4 + [jax.ShapeDtypeStruct((EXPERTS, tokens, kept), BF)],
        [IN_HBM] * 5,
        weight_scratch(w1, w2)
        + [pltpu.VMEM((EXPERTS, most, dim), BF)] * 2
        + [pltpu.VMEM((EXPERTS, most, 2 * dim), BF), pltpu.VMEM((2, ROWS, kept), BF), pltpu.VMEM((4, tok + 8, dim), F32)]
        + [pltpu.SemaphoreType.DMA((EXPERTS, 3)), pltpu.SemaphoreType.DMA((2,)), pltpu.SemaphoreType.DMA((4,))],
        2 * 6 * tokens * dim * width,
    )
    return out[:4], out[4]


def run_dw(kept, maps, shape1, shape2):
    tokens = kept.shape[1]
    return call(
        dw_kernel, (maps[0], kept),
        [IN_SMEM, IN_HBM],
        [jax.ShapeDtypeStruct(shape1, F32), jax.ShapeDtypeStruct(shape1, F32), jax.ShapeDtypeStruct(shape2, F32)],
        [IN_HBM] * 3,
        [pltpu.VMEM((2, 2 * ROWS, kept.shape[2]), BF), pltpu.VMEM(shape1, F32), pltpu.VMEM(shape1, F32), pltpu.VMEM(shape2, F32)]
        + [pltpu.SemaphoreType.DMA((2,)), pltpu.SemaphoreType.DMA((EXPERTS, 3))],
        2 * 3 * tokens * shape1[1] * shape1[2],
    )


def solution(mesh):
    tok_spec = P(("dp", "ep"))
    w_spec = P("ep")
    across = [(0, 2), (2, 0), (1, 3), (3, 1)]
    beside = [(0, 1), (1, 0), (2, 3), (3, 2)]
    cross = [(0, 3), (3, 0), (1, 2), (2, 1)]

    def permute(v, pairs):
        return lax.ppermute(v, "ep", pairs)

    def gather(own):
        other = permute(own, across)
        return other, permute(other, beside), own, permute(own, beside)

    def gather_direct(own):
        return permute(own, across), permute(own, cross), own, permute(own, beside)

    def combine(parts):
        other, diagonal, own, mate = parts
        theirs = other + permute(diagonal, beside)
        return own + permute(mate, beside) + permute(theirs, across)

    def device_program(x_in, idx_a, idx_b, gate_a, gate_b, dy_out, w1_a, w3_a, w2_a, w1_b, w3_b, w2_b):
        tok, top_k = idx_a.shape
        own_map = jnp.concatenate([idx_a.astype(F32), idx_b.astype(F32), gate_a, gate_b], axis=1).T
        x_all, (maps_a, maps_b, maps_far, maps_near) = run_gather(own_map, x_in)

        def add(base, total):
            return (base.astype(F32) + total[:tok]).astype(BF)

        def dgate_of(total):
            return total[tok : tok + top_k].T

        dy_own, x_other = lax.optimization_barrier((dy_out, x_all[0]))
        x_all = (x_other, *x_all[1:])
        dy_all = gather(dy_own)
        far_parts = run_forward(x_all[:2], maps_far, w1_a, w3_a, w2_a)
        near_parts = run_forward(x_all[2:], maps_near, w1_a, w3_a, w2_a)
        x_mid = add(x_in, combine((*far_parts, *near_parts)))
        mid_all = gather(x_mid)
        x_again, mid_other = lax.optimization_barrier((x_in, mid_all[0]))
        mid_all = (mid_other, *mid_all[1:])
        again_all = gather_direct(x_again)
        dx_parts, kept_b = run_dx(mid_all, dy_all, maps_b, w1_b, w3_b, w2_b)
        total = combine(dx_parts)
        dx_mid, dgate_b = add(dy_out, total), dgate_of(total)
        dmid_all = gather_direct(dx_mid)
        x_out = add(x_mid, combine(run_forward(mid_all, maps_b, w1_b, w3_b, w2_b)))
        grads_b = run_dw(kept_b, maps_b, w1_b.shape, w2_b.shape)
        dx_parts, kept_a = run_dx(again_all, dmid_all, maps_a, w1_a, w3_a, w2_a)
        total = combine(dx_parts)
        dx_in, dgate_a = add(dx_mid, total), dgate_of(total)
        grads_a = run_dw(kept_a, maps_a, w1_a.shape, w2_a.shape)
        return (x_out, dx_in, *grads_a, *grads_b, dgate_a, dgate_b)


    return jax.shard_map(device_program, mesh=mesh, in_specs=(tok_spec,) * 6 + (w_spec,) * 6, out_specs=(tok_spec,) * 10, check_vma=False)
```

profile of v0, /device:TPU:0, one launch (start us, length us, event | category | flops | bytes accessed | tf_op | source)
XLA Modules:
  0.0 327.8 jit_solution(12128926196592227633)
XLA Ops:
  2.0 1.3 maximum_bitcast_fusion.map_ref
  3.3 19.5 %gather_slots.1 = (bf16[512,512]{1,0:T(8,128)(2,1)}, bf16[512,512]{1,0:T(8,128)(2,1)}, bf16[512,512]{1,0:T(8,128)(2,1)}, s32[2,128]{1,0:T(2,128)}, f32[2,2048]{1...) custom-call(f32[8,512]{1,0:T(8,128)} %maximum_bitcast_fusion.map_ref, ...), custom_call_target="tpu_custom_call" | custom-call | flops 10000000 | bytes 4000000 | tf_op jit(solution)/shard_map/gather_slots/pallas_call | solution.py:445
  22.8 9.3 %shard_map.196 = (f32[512,512]{1,0:T(8,128)}, f32[512,512]{1,0:T(8,128)}) custom-call(s32[2,128]{1,0:T(2,128)} %get-tuple-element.59.starts_ref, bf16[512,512]{1,0:T(8,128)(2,1)} %get-tuple-element.61.refs_0_, bf16[512,512]{1,0:T(8,128)(2,1)} %get-tuple-element.62.refs_1_, f32[2,1024]{1,0:T(2,128)} %get-tuple-element.63.refs_2_, ...), custom_call_target="tpu_custom_call" | custom-call | flops 5637144576 | bytes 40000000 | tf_op jit(solution)/shard_map/pallas_call | solution.py:424
  32.7 9.3 %shard_map.195 = (f32[512,512]{1,0:T(8,128)}, f32[512,512]{1,0:T(8,128)}) custom-call(s32[2,128]{1,0:T(2,128)} %get-tuple-element.53.starts_ref, bf16[512,512]{1,0:T(8,128)(2,1)} %x2, bf16[512,512]{1,0:T(8,128)(2,1)} %get-tuple-element.54.refs_1_, f32[2,1024]{1,0:T(2,128)} %get-tuple-element.55.refs_2_, f32[1024,8]{1,0:T(8,128)} %get-tuple-element.56.refs_3_, ...), custom_call_target="tpu_custom_call" | custom-call | flops 5637144576 | bytes 40000000 | tf_op jit(solution)/shard_map/pallas_call | solution.py:424
  42.1 1.9 add.49
  44.0 10.3 %collective-permute-start.2 = (f32[512,512]{1,0:T(8,128)S(1)}, f32[512,512]{1,0:T(8,128)S(1)}, u32[]{:S(2)}, u32[]{:S(2)}) collective-permute-start(f32[512,512]{1,0:T(8,128)S(1)} %add.49), channel_id=1, source_target_pairs={{0,2},{2,0},{1,3},{3,1},{4,6},{6,4},{5,7},{7,5}} | collective-permute-start | bytes 3145736 | tf_op jit(solution)/shard_map/ppermute | solution.py:524
  54.3 24.0 %collective-permute-done.2 = f32[512,512]{1,0:T(8,128)S(1)} collective-permute-done((f32[512,512]{1,0:T(8,128)S(1)}, f32[512,512]{1,0:T(8,128)S(1)}, u32[]{:S(2)}, u32[]{:S(2)}) %collective-permute-start.2) | collective-permute-done | bytes 1048608 | tf_op jit(solution)/shard_map/ppermute | solution.py:524
  78.3 1.5 add_convert_fusion.1.refs_2_.x2
  79.8 2.0 collective-permute-start.3
  81.8 7.7 %collective-permute-done.9.g0 = bf16[512,512]{1,0:T(8,128)(2,1)S(1)} collective-permute-done((bf16[512,512]{1,0:T(8,128)(2,1)S(1)}, bf16[512,512]{1,0:T(8,128)(2,1)S(1)}, u32[]{:S(2)}, u32[]{:S(2)}) %collective-permute-start.9) | collective-permute-done | bytes 524320 | tf_op jit(solution)/shard_map/ppermute | solution.py:524
  90.0 10.5 %collective-permute-done.3.refs_0_.x0 = bf16[512,512]{1,0:T(8,128)(2,1)S(1)} collective-permute-done((bf16[512,512]{1,0:T(8,128)(2,1)S(1)}, bf16[512,512]{1,0:T(8,128)(2,1)S(1)}, u32[]{:S(2)}, u32[]{:S(2)}) %collective-permute-start.3) | collective-permute-done | bytes 524320 | tf_op jit(solution)/shard_map/ppermute | solution.py:524
  103.2 24.5 %shard_map.198 = (f32[520,512]{1,0:T(8,128)}, f32[520,512]{1,0:T(8,128)}, f32[520,512]{1,0:T(8,128)}, f32[520,512]{1,0:T(8,128)}, bf16[2,2048,6400]{2,1,0:T(8,128)(2,1)}) custom-call(s32[2,128]{1,0:T(2,128)} %get-tuple-element.67.starts_ref, bf16[512,512]{1,0:T(8,128)(2,1)} %copy-done.12, bf16[512,512]{1,0:T(8,128)(2,1)} %copy-done.17, ...), custom_call_target="tpu_custom_call" | custom-call | flops 22548578304 | bytes 40000000 | tf_op jit(solution)/shard_map/pallas_call | solution.py:424
  128.2 2.4 collective-permute-done.13
  130.6 2.4 add.57
  133.0 20.5 %collective-permute-start.14 = (f32[520,512]{1,0:T(8,128)}, f32[520,512]{1,0:T(8,128)}, u32[]{:S(2)}, u32[]{:S(2)}) collective-permute-start(f32[520,512]{1,0:T(8,128)} %add.57), channel_id=1, source_target_pairs={{0,2},{2,0},{1,3},{3,1},{4,6},{6,4},{5,7},{7,5}} | collective-permute-start | bytes 3194888 | tf_op jit(solution)/shard_map/ppermute | solution.py:524
  153.6 14.0 %shard_map.197 = (f32[512,512]{1,0:T(8,128)}, f32[512,512]{1,0:T(8,128)}, f32[512,512]{1,0:T(8,128)}, f32[512,512]{1,0:T(8,128)}) custom-call(s32[2,128]{1,0:T(2,128)} %get-tuple-element.67.starts_ref, bf16[512,512]{1,0:T(8,128)(2,1)} %copy-done.12, bf16[512,512]{1,0:T(8,128)(2,1)} %copy-done.17, bf16[512,512]{1,0:T(8,128)(2,1)} %copy-done.3, ...), custom_call_target="tpu_custom_call" | custom-call | flops 11274289152 | bytes 40000000 | tf_op jit(solution)/shard_map/pallas_call | solution.py:424
  168.1 9.2 %collective-permute-start.16 = (bf16[512,512]{1,0:T(8,128)(2,1)}, bf16[512,512]{1,0:T(8,128)(2,1)S(1)}, u32[]{:S(2)}, u32[]{:S(2)}) collective-permute-start(bf16[512,512]{1,0:T(8,128)(2,1)} %x2), channel_id=1, source_target_pairs={{0,3},{3,0},{1,2},{2,1},{4,7},{7,4},{5,6},{6,5}} | collective-permute-start | bytes 1572872 | tf_op jit(solution)/shard_map/ppermute | solution.py:524
  177.7 2.3 add_add_fusion.1
  180.4 1.7 collective-permute-start.19
  183.6 6.4 %collective-permute-done.16.x1 = bf16[512,512]{1,0:T(8,128)(2,1)S(1)} collective-permute-done((bf16[512,512]{1,0:T(8,128)(2,1)}, bf16[512,512]{1,0:T(8,128)(2,1)S(1)}, u32[]{:S(2)}, u32[]{:S(2)}) %collective-permute-start.16) | collective-permute-done | bytes 524320 | tf_op jit(solution)/shard_map/ppermute | solution.py:524
  190.5 11.4 %collective-permute-done.15.x0 = bf16[512,512]{1,0:T(8,128)(2,1)S(1)} collective-permute-done((bf16[512,512]{1,0:T(8,128)(2,1)}, bf16[512,512]{1,0:T(8,128)(2,1)S(1)}, u32[]{:S(2)}, u32[]{:S(2)}) %collective-permute-start.15) | collective-permute-done | bytes 524320 | tf_op jit(solution)/shard_map/ppermute | solution.py:524
  201.9 1.7 collective-permute-start.8
  203.6 8.7 %collective-permute-done.19.g1 = bf16[512,512]{1,0:T(8,128)(2,1)S(1)} collective-permute-done((bf16[512,512]{1,0:T(8,128)(2,1)S(1)}, bf16[512,512]{1,0:T(8,128)(2,1)S(1)}, u32[]{:S(2)}, u32[]{:S(2)}) %collective-permute-start.19) | collective-permute-done | bytes 524320 | tf_op jit(solution)/shard_map/ppermute | solution.py:524
  212.4 12.1 %collective-permute-done.18.g0 = bf16[512,512]{1,0:T(8,128)(2,1)S(1)} collective-permute-done((bf16[512,512]{1,0:T(8,128)(2,1)S(1)}, bf16[512,512]{1,0:T(8,128)(2,1)S(1)}, u32[]{:S(2)}, u32[]{:S(2)}) %collective-permute-start.18) | collective-permute-done | bytes 524320 | tf_op jit(solution)/shard_map/ppermute | solution.py:524
  225.2 24.7 %shard_map.199 = (f32[520,512]{1,0:T(8,128)}, f32[520,512]{1,0:T(8,128)}, f32[520,512]{1,0:T(8,128)}, f32[520,512]{1,0:T(8,128)}, bf16[2,2048,6400]{2,1,0:T(8,128)(2,1)}) custom-call(s32[2,128]{1,0:T(2,128)} %get-tuple-element.80.starts_ref, bf16[512,512]{1,0:T(8,128)(2,1)} %copy-done.13, bf16[512,512]{1,0:T(8,128)(2,1)} %copy-done.11, bf16[512,512]{1,0:T(8,128)(2,1)} %x2, ...), custom_call_target="tpu_custom_call" | custom-call | flops 22548578304 | bytes 40000000 | tf_op jit(solution)/shard_map/pallas_call | solution.py:424
  250.0 14.2 %shard_map.201 = (f32[2,512,1792]{2,1,0:T(8,128)}, f32[2,512,1792]{2,1,0:T(8,128)}, f32[2,1792,512]{2,1,0:T(8,128)}) custom-call(s32[2,128]{1,0:T(2,128)} %get-tuple-element.67.starts_ref, bf16[2,2048,6400]{2,1,0:T(8,128)(2,1)} %get-tuple-element.92.kept_hbm), custom_call_target="tpu_custom_call" | custom-call | flops 11274289152 | bytes 40000000 | tf_op jit(solution)/shard_map/pallas_call | solution.py:424
  264.2 3.2 add_convert_fusion
  267.8 2.4 add.61
  270.3 29.2 %collective-permute-start.23 = (f32[520,512]{1,0:T(8,128)}, f32[520,512]{1,0:T(8,128)}, u32[]{:S(2)}, u32[]{:S(2)}) collective-permute-start(f32[520,512]{1,0:T(8,128)} %add.61), channel_id=1, source_target_pairs={{0,2},{2,0},{1,3},{3,1},{4,6},{6,4},{5,7},{7,5}} | collective-permute-start | bytes 3194888 | tf_op jit(solution)/shard_map/ppermute | solution.py:524
  300.8 14.0 %shard_map.200 = (f32[2,512,1792]{2,1,0:T(8,128)}, f32[2,512,1792]{2,1,0:T(8,128)}, f32[2,1792,512]{2,1,0:T(8,128)}) custom-call(s32[2,128]{1,0:T(2,128)} %get-tuple-element.80.starts_ref, bf16[2,2048,6400]{2,1,0:T(8,128)(2,1)} %get-tuple-element.88.kept_hbm), custom_call_target="tpu_custom_call" | custom-call | flops 11274289152 | bytes 40000000 | tf_op jit(solution)/shard_map/pallas_call | solution.py:424
  314.9 9.1 %collective-permute-done.23 = f32[520,512]{1,0:T(8,128)} collective-permute-done((f32[520,512]{1,0:T(8,128)}, f32[520,512]{1,0:T(8,128)}, u32[]{:S(2)}, u32[]{:S(2)}) %collective-permute-start.23) | collective-permute-done | bytes 1064992 | tf_op jit(solution)/shard_map/ppermute | solution.py:524
  324.0 2.3 add_add_fusion
  (83 shorter events, 13.3 us)
Async XLA Ops:
  32.1 10.0 %collective-permute-start.1 = (f32[512,512]{1,0:T(8,128)}, f32[512,512]{1,0:T(8,128)}, u32[]{:S(2)}, u32[]{:S(2)}) collective-permute-start(f32[512,512]{1,0:T(8,128)} %get-tuple-element.66), channel_id=1, source_target_pairs={{0,1},{1,0},{2,3},{3,2},{4,5},{5,4},{6,7},{7,6}} | collective-permute-start | bytes 3145736 | tf_op jit(solution)/shard_map/ppermute | solution.py:524
  42.0 12.2 %collective-permute-start = (f32[512,512]{1,0:T(8,128)}, f32[512,512]{1,0:T(8,128)S(1)}, u32[]{:S(2)}, u32[]{:S(2)}) collective-permute-start(f32[512,512]{1,0:T(8,128)} %get-tuple-element.58), channel_id=1, source_target_pairs={{0,1},{1,0},{2,3},{3,2},{4,5},{5,4},{6,7},{7,6}} | collective-permute-start | bytes 3145736 | tf_op jit(solution)/shard_map/ppermute | solution.py:524
  42.1 12.2 %copy-start.8 = (bf16[512,512]{1,0:T(8,128)(2,1)S(1)}, bf16[512,512]{1,0:T(8,128)(2,1)}, u32[]{:S(2)}) copy-start(bf16[512,512]{1,0:T(8,128)(2,1)} %g2) | copy-start | bytes 1572868
  42.1 36.1 %copy-start.7 = (f32[512,512]{1,0:T(8,128)S(1)}, f32[512,512]{1,0:T(8,128)}, u32[]{:S(2)}) copy-start(f32[512,512]{1,0:T(8,128)} %get-tuple-element.57) | copy-start | bytes 3145732
  44.0 34.3 %collective-permute-start.2 = (f32[512,512]{1,0:T(8,128)S(1)}, f32[512,512]{1,0:T(8,128)S(1)}, u32[]{:S(2)}, u32[]{:S(2)}) collective-permute-start(f32[512,512]{1,0:T(8,128)S(1)} %add.49), channel_id=1, source_target_pairs={{0,2},{2,0},{1,3},{3,1},{4,6},{6,4},{5,7},{7,5}} | collective-permute-start | bytes 3145736 | tf_op jit(solution)/shard_map/ppermute | solution.py:524
  54.2 35.2 %collective-permute-start.9 = (bf16[512,512]{1,0:T(8,128)(2,1)S(1)}, bf16[512,512]{1,0:T(8,128)(2,1)S(1)}, u32[]{:S(2)}, u32[]{:S(2)}) collective-permute-start(bf16[512,512]{1,0:T(8,128)(2,1)S(1)} %copy-done.8), channel_id=1, source_target_pairs={{0,2},{2,0},{1,3},{3,1},{4,6},{6,4},{5,7},{7,5}} | collective-permute-start | bytes 1572872 | tf_op jit(solution)/shard_map/ppermute | solution.py:524
  79.8 23.5 %copy-start.3 = (bf16[512,512]{1,0:T(8,128)(2,1)}, bf16[512,512]{1,0:T(8,128)(2,1)S(1)}, u32[]{:S(2)}) copy-start(bf16[512,512]{1,0:T(8,128)(2,1)S(1)} %add_convert_fusion.1.refs_2_.x2) | copy-start | bytes 1572868
  79.8 20.7 %collective-permute-start.3 = (bf16[512,512]{1,0:T(8,128)(2,1)S(1)}, bf16[512,512]{1,0:T(8,128)(2,1)S(1)}, u32[]{:S(2)}, u32[]{:S(2)}) collective-permute-start(bf16[512,512]{1,0:T(8,128)(2,1)S(1)} %add_convert_fusion.1.refs_2_.x2), channel_id=1, source_target_pairs={{0,2},{2,0},{1,3},{3,1},{4,6},{6,4},{5,7},{7,5}} | collective-permute-start | bytes 1572872 | tf_op jit(solution)/shard_map/ppermute | solution.py:524
  81.8 18.7 %collective-permute-start.11 = (bf16[512,512]{1,0:T(8,128)(2,1)S(1)}, bf16[512,512]{1,0:T(8,128)(2,1)S(1)}, u32[]{:S(2)}, u32[]{:S(2)}) collective-permute-start(bf16[512,512]{1,0:T(8,128)(2,1)S(1)} %copy-done.8), channel_id=1, source_target_pairs={{0,1},{1,0},{2,3},{3,2},{4,5},{5,4},{6,7},{7,6}} | collective-permute-start | bytes 1572872 | tf_op jit(solution)/shard_map/ppermute | solution.py:524
  89.5 12.9 %copy-start.14 = (bf16[512,512]{1,0:T(8,128)(2,1)}, bf16[512,512]{1,0:T(8,128)(2,1)S(1)}, u32[]{:S(2)}) copy-start(bf16[512,512]{1,0:T(8,128)(2,1)S(1)} %collective-permute-done.9.g0) | copy-start | bytes 1572868
  89.5 11.0 %collective-permute-start.10 = (bf16[512,512]{1,0:T(8,128)(2,1)S(1)}, bf16[512,512]{1,0:T(8,128)(2,1)S(1)}, u32[]{:S(2)}, u32[]{:S(2)}) collective-permute-start(bf16[512,512]{1,0:T(8,128)(2,1)S(1)} %collective-permute-done.9.g0), channel_id=1, source_target_pairs={{0,1},{1,0},{2,3},{3,2},{4,5},{5,4},{6,7},{7,6}} | collective-permute-start | bytes 1572872 | tf_op jit(solution)/shard_map/ppermute | solution.py:524
  89.5 11.1 %collective-permute-start.5 = (bf16[512,512]{1,0:T(8,128)(2,1)S(1)}, bf16[512,512]{1,0:T(8,128)(2,1)S(1)}, u32[]{:S(2)}, u32[]{:S(2)}) collective-permute-start(bf16[512,512]{1,0:T(8,128)(2,1)S(1)} %add_convert_fusion.1.refs_2_.x2), channel_id=1, source_target_pairs={{0,1},{1,0},{2,3},{3,2},{4,5},{5,4},{6,7},{7,6}} | collective-permute-start | bytes 1572872 | tf_op jit(solution)/shard_map/ppermute | solution.py:524
  100.5 1.9 collective-permute-start.4
  127.7 2.9 collective-permute-start.13
  127.8 49.5 %collective-permute-start.12 = (f32[520,512]{1,0:T(8,128)}, f32[520,512]{1,0:T(8,128)}, u32[]{:S(2)}, u32[]{:S(2)}) collective-permute-start(f32[520,512]{1,0:T(8,128)} %get-tuple-element.77), channel_id=1, source_target_pairs={{0,1},{1,0},{2,3},{3,2},{4,5},{5,4},{6,7},{7,6}} | collective-permute-start | bytes 3194888 | tf_op jit(solution)/shard_map/ppermute | solution.py:524
  133.0 44.7 %collective-permute-start.14 = (f32[520,512]{1,0:T(8,128)}, f32[520,512]{1,0:T(8,128)}, u32[]{:S(2)}, u32[]{:S(2)}) collective-permute-start(f32[520,512]{1,0:T(8,128)} %add.57), channel_id=1, source_target_pairs={{0,2},{2,0},{1,3},{3,1},{4,6},{6,4},{5,7},{7,5}} | collective-permute-start | bytes 3194888 | tf_op jit(solution)/shard_map/ppermute | solution.py:524
  167.6 14.5 %collective-permute-start.7 = (f32[512,512]{1,0:T(8,128)}, f32[512,512]{1,0:T(8,128)S(1)}, u32[]{:S(2)}, u32[]{:S(2)}) collective-permute-start(f32[512,512]{1,0:T(8,128)} %get-tuple-element.74), channel_id=1, source_target_pairs={{0,1},{1,0},{2,3},{3,2},{4,5},{5,4},{6,7},{7,6}} | collective-permute-start | bytes 3145736 | tf_op jit(solution)/shard_map/ppermute | solution.py:524
  167.6 12.7 %collective-permute-start.17 = (bf16[512,512]{1,0:T(8,128)(2,1)}, bf16[512,512]{1,0:T(8,128)(2,1)S(1)}, u32[]{:S(2)}, u32[]{:S(2)}) collective-permute-start(bf16[512,512]{1,0:T(8,128)(2,1)} %x2), channel_id=1, source_target_pairs={{0,1},{1,0},{2,3},{3,2},{4,5},{5,4},{6,7},{7,6}} | collective-permute-start | bytes 1572872 | tf_op jit(solution)/shard_map/ppermute | solution.py:524
  168.1 21.8 %collective-permute-start.16 = (bf16[512,512]{1,0:T(8,128)(2,1)}, bf16[512,512]{1,0:T(8,128)(2,1)S(1)}, u32[]{:S(2)}, u32[]{:S(2)}) collective-permute-start(bf16[512,512]{1,0:T(8,128)(2,1)} %x2), channel_id=1, source_target_pairs={{0,3},{3,0},{1,2},{2,1},{4,7},{7,4},{5,6},{6,5}} | collective-permute-start | bytes 1572872 | tf_op jit(solution)/shard_map/ppermute | solution.py:524
  177.4 24.6 %collective-permute-start.15 = (bf16[512,512]{1,0:T(8,128)(2,1)}, bf16[512,512]{1,0:T(8,128)(2,1)S(1)}, u32[]{:S(2)}, u32[]{:S(2)}) collective-permute-start(bf16[512,512]{1,0:T(8,128)(2,1)} %x2), channel_id=1, source_target_pairs={{0,2},{2,0},{1,3},{3,1},{4,6},{6,4},{5,7},{7,5}} | collective-permute-start | bytes 1572872 | tf_op jit(solution)/shard_map/ppermute | solution.py:524
  180.2 23.4 %collective-permute-start.20 = (bf16[512,512]{1,0:T(8,128)(2,1)S(1)}, bf16[512,512]{1,0:T(8,128)(2,1)S(1)}, u32[]{:S(2)}, u32[]{:S(2)}) collective-permute-start(bf16[512,512]{1,0:T(8,128)(2,1)S(1)} %fusion.1.g2), channel_id=1, source_target_pairs={{0,1},{1,0},{2,3},{3,2},{4,5},{5,4},{6,7},{7,6}} | collective-permute-start | bytes 1572872 | tf_op jit(solution)/shard_map/ppermute | solution.py:524
  180.4 32.0 %collective-permute-start.19 = (bf16[512,512]{1,0:T(8,128)(2,1)S(1)}, bf16[512,512]{1,0:T(8,128)(2,1)S(1)}, u32[]{:S(2)}, u32[]{:S(2)}) collective-permute-start(bf16[512,512]{1,0:T(8,128)(2,1)S(1)} %fusion.1.g2), channel_id=1, source_target_pairs={{0,3},{3,0},{1,2},{2,1},{4,7},{7,4},{5,6},{6,5}} | collective-permute-start | bytes 1572872 | tf_op jit(solution)/shard_map/ppermute | solution.py:524
  182.1 42.3 %collective-permute-start.18 = (bf16[512,512]{1,0:T(8,128)(2,1)S(1)}, bf16[512,512]{1,0:T(8,128)(2,1)S(1)}, u32[]{:S(2)}, u32[]{:S(2)}) collective-permute-start(bf16[512,512]{1,0:T(8,128)(2,1)S(1)} %fusion.1.g2), channel_id=1, source_target_pairs={{0,2},{2,0},{1,3},{3,1},{4,6},{6,4},{5,7},{7,5}} | collective-permute-start | bytes 1572872 | tf_op jit(solution)/shard_map/ppermute | solution.py:524
  190.0 34.4 %copy-start.11 = (bf16[512,512]{1,0:T(8,128)(2,1)}, bf16[512,512]{1,0:T(8,128)(2,1)S(1)}, u32[]{:S(2)}) copy-start(bf16[512,512]{1,0:T(8,128)(2,1)S(1)} %collective-permute-done.16.x1) | copy-start | bytes 1572868
  190.0 74.2 %collective-permute-start.6 = (f32[512,512]{1,0:T(8,128)}, f32[512,512]{1,0:T(8,128)}, u32[]{:S(2)}, u32[]{:S(2)}) collective-permute-start(f32[512,512]{1,0:T(8,128)} %get-tuple-element.72), channel_id=1, source_target_pairs={{0,1},{1,0},{2,3},{3,2},{4,5},{5,4},{6,7},{7,6}} | collective-permute-start | bytes 3145736 | tf_op jit(solution)/shard_map/ppermute | solution.py:524
  201.9 22.5 %copy-start.13 = (bf16[512,512]{1,0:T(8,128)(2,1)}, bf16[512,512]{1,0:T(8,128)(2,1)S(1)}, u32[]{:S(2)}) copy-start(bf16[512,512]{1,0:T(8,128)(2,1)S(1)} %collective-permute-done.15.x0) | copy-start | bytes 1572868
  201.9 62.2 %collective-permute-start.8 = (f32[512,512]{1,0:T(8,128)}, f32[512,512]{1,0:T(8,128)}, u32[]{:S(2)}, u32[]{:S(2)}) collective-permute-start(f32[512,512]{1,0:T(8,128)} %add.53), channel_id=1, source_target_pairs={{0,2},{2,0},{1,3},{3,1},{4,6},{6,4},{5,7},{7,5}} | collective-permute-start | bytes 3145736 | tf_op jit(solution)/shard_map/ppermute | solution.py:524
  203.6 20.8 %copy-start.16 = (bf16[512,512]{1,0:T(8,128)(2,1)}, bf16[512,512]{1,0:T(8,128)(2,1)S(1)}, u32[]{:S(2)}) copy-start(bf16[512,512]{1,0:T(8,128)(2,1)S(1)} %collective-permute-done.20.g3) | copy-start | bytes 1572868
  249.9 17.9 %collective-permute-start.22 = (f32[520,512]{1,0:T(8,128)}, f32[520,512]{1,0:T(8,128)}, u32[]{:S(2)}, u32[]{:S(2)}) collective-permute-start(f32[520,512]{1,0:T(8,128)} %get-tuple-element.87), channel_id=1, source_target_pairs={{0,1},{1,0},{2,3},{3,2},{4,5},{5,4},{6,7},{7,6}} | collective-permute-start | bytes 3194888 | tf_op jit(solution)/shard_map/ppermute | solution.py:524
  249.9 14.2 %copy-start.4 = (bf16[512,512]{1,0:T(8,128)(2,1)S(1)}, bf16[512,512]{1,0:T(8,128)(2,1)}, u32[]{:S(2)}) copy-start(bf16[512,512]{1,0:T(8,128)(2,1)} %copy-done.3) | copy-start | bytes 1572868
  267.3 47.5 %collective-permute-start.21 = (f32[520,512]{1,0:T(8,128)}, f32[520,512]{1,0:T(8,128)}, u32[]{:S(2)}, u32[]{:S(2)}) collective-permute-start(f32[520,512]{1,0:T(8,128)} %get-tuple-element.85), channel_id=1, source_target_pairs={{0,1},{1,0},{2,3},{3,2},{4,5},{5,4},{6,7},{7,6}} | collective-permute-start | bytes 3194888 | tf_op jit(solution)/shard_map/ppermute | solution.py:524
  270.3 53.7 %collective-permute-start.23 = (f32[520,512]{1,0:T(8,128)}, f32[520,512]{1,0:T(8,128)}, u32[]{:S(2)}, u32[]{:S(2)}) collective-permute-start(f32[520,512]{1,0:T(8,128)} %add.61), channel_id=1, source_target_pairs={{0,2},{2,0},{1,3},{3,1},{4,6},{6,4},{5,7},{7,5}} | collective-permute-start | bytes 3194888 | tf_op jit(solution)/shard_map/ppermute | solution.py:524
  (14 other events, 40.2 us)
where the time goes:
time: 328 us
  Pallas kernels  129 us (39%)
  waiting for transfers between devices  93.4 us (28%)
  starting transfers between devices  78.8 us (24%)
  other arithmetic  21 us (6%)
  local copies, waits for them, and re-layouts  4.28 us (1%)
    pallas_call x7, Pallas kernels, call(): pl.pallas_call(kernel, in_specs=in_specs, out_specs=out_specs, out_shape=...  110 us
    ppermute x24, waiting for transfers between devices, permute(): return lax.ppermute(v, 'ep', pairs)  93.4 us
    ppermute x24, starting transfers between devices, permute(): return lax.ppermute(v, 'ep', pairs)  78.8 us
    pallas_call x1, Pallas kernels, run_gather(): pl.pallas_call(gather_kernel, in_specs=[IN_VMEM] * 2, out_specs=[IN_HBM]...  19.5 us
    add x4, other arithmetic, combine(): theirs = other + permute(diagonal, beside)  7.91 us
  transfers between devices with their start and end apart: 24, of which 10 were waited for; matrix products, arithmetic and copies ran while one was open for 5% of the time, Pallas kernels for 23%

commit v1 on v0

--- a/solution.py
+++ b/solution.py
@@ -200,9 +200,9 @@
     return [pltpu.make_async_copy(h.at[e], v.at[e], sems.at[e, i]) for i, (h, v) in enumerate(zip(hbm, vmem))]
 
 
-def forward_kernel(n, starts_ref, *refs):
-    xs, (rows_ref, cols_ref, w1_hbm, w3_hbm, w2_hbm), ys = refs[:n], refs[n : n + 5], refs[n + 5 : 2 * n + 5]
-    w1, w3, w2, u_all, o_all, h_ref, y_buf, w_sems, y_sems = refs[2 * n + 5 :]
+def forward_kernel(n, m, starts_ref, *refs):
+    xs, (rows_ref, cols_ref, w1_hbm, w3_hbm, w2_hbm), ys = refs[:n], refs[n : n + 5], refs[n + 5 : n + m + 5]
+    w1, w3, w2, u_all, o_all, h_ref, y_buf, w_sems, y_sems = refs[n + m + 5 :]
     blocks = rows_ref.shape[1] // TOKS
     width = w1.shape[2]
     slots = Slots(starts_ref, rows_ref, cols_ref, blocks)
@@ -255,10 +255,11 @@
         pltpu.make_async_copy(y_buf.at[n], ref, y_sems.at[n]).wait()
 
 
-def dx_kernel(starts_ref, x0, x1, x2, x3, g0, g1, g2, g3, rows_ref, cols_ref, w1_hbm, w3_hbm, w2_hbm,
-              dx0, dx1, dx2, dx3, kept_hbm, w1, w3, w2, u_all, q_all, od_all, kept, dx_buf, w_sems, k_sems, dx_sems):
-    xs, gs, dxs = (x0, x1, x2, x3), (g0, g1, g2, g3), (dx0, dx1, dx2, dx3)
-    tok = x0.shape[0]
+def dx_kernel(n, starts_ref, *refs):
+    xs, gs, (rows_ref, cols_ref, w1_hbm, w3_hbm, w2_hbm) = refs[:n], refs[n : n + 4], refs[n + 4 : n + 9]
+    dxs, kept_hbm = refs[n + 9 : n + 13], refs[n + 13]
+    w1, w3, w2, u_all, q_all, od_all, kept, dx_buf, w_sems, k_sems, dx_sems = refs[n + 14 :]
+    tok = gs[0].shape[0]
     blocks = rows_ref.shape[1] // TOKS
     dim, width = w1.shape[1:]
     slots = Slots(starts_ref, rows_ref, cols_ref, blocks)
@@ -280,20 +281,20 @@
 
     lax.fori_loop(0, EXPERTS, gather_rows, 0)
 
-    def copy_out(e, k):
-        return pltpu.make_async_copy(kept.at[lax.rem(k, 2)], kept_hbm.at[e, tile_rows(k), :], k_sems.at[lax.rem(k, 2)])
+    def copy_out(e, k, slot):
+        return pltpu.make_async_copy(kept.at[slot], kept_hbm.at[e, tile_rows(k), :], k_sems.at[slot])
 
     def expert(e, carry):
         for copy in weight_copies((w1_hbm, w3_hbm, w2_hbm), (w1, w3, w2), w_sems, e):
             copy.wait()
-        count = slots.tiles(e)
+        before = e * slots.tiles(0)
 
         def tile(k, inner):
-            slot = lax.rem(k, 2)
-
-            @pl.when(k >= 2)
+            slot = lax.rem(before + k, 2)
+
+            @pl.when(before + k >= 2)
             def _():
-                copy_out(e, k - 2).wait()
+                copy_out(e, k, slot).wait()
 
             u = u_all[e, tile_rows(k), :]
             q = q_all[e, tile_rows(k), :]
@@ -312,19 +313,10 @@
             od_all[e, tile_rows(k), :dim] = mm(kept[slot, :, :width], w2[e]).astype(BF)
             du = mm_nt(kept[slot, :, width : 2 * width], w1[e]) + mm_nt(kept[slot, :, 2 * width : 3 * width], w3[e])
             od_all[e, tile_rows(k), dim:] = du.astype(BF)
-            copy_out(e, k).start()
+            copy_out(e, k, slot).start()
             return inner
 
-        lax.fori_loop(0, count, tile, 0)
-
-        @pl.when(count >= 2)
-        def _():
-            copy_out(e, count - 2).wait()
-
-        @pl.when(count >= 1)
-        def _():
-            copy_out(e, count - 1).wait()
-
+        lax.fori_loop(0, slots.tiles(e), tile, 0)
         return carry
 
     lax.fori_loop(0, EXPERTS, expert, 0)
@@ -351,6 +343,8 @@
         copies[-1].start()
     for copy in copies:
         copy.wait()
+    for slot in range(2):
+        copy_out(0, 0, slot).wait()
 
 
 def dw_kernel(starts_ref, kept_hbm, dw1_hbm, dw3_hbm, dw2_hbm, kept, dw1, dw3, dw2, k_sems, o_sems):
@@ -462,33 +456,34 @@
     return [pltpu.VMEM(w1.shape, BF), pltpu.VMEM(w1.shape, BF), pltpu.VMEM(w2.shape, BF)]
 
 
-def run_forward(xs, maps, w1, w3, w2):
-    tok, dim = xs[0].shape
-    tokens = tok * len(xs)
+def run_forward(tok, xs, maps, w1, w3, w2):
+    dim = xs[0].shape[1]
+    tokens = sum(x.shape[0] for x in xs)
+    parts = tokens // tok
     width = w1.shape[2]
     most = tokens + TOKS + ALIGN + ROWS
     return call(
-        functools.partial(forward_kernel, len(xs)), (maps[0], *xs, maps[1], maps[2], w1, w3, w2),
+        functools.partial(forward_kernel, len(xs), parts), (maps[0], *xs, maps[1], maps[2], w1, w3, w2),
         [IN_SMEM] + [IN_VMEM] * (len(xs) + 2) + [IN_HBM] * 3,
-        [jax.ShapeDtypeStruct((tok, dim), F32)] * len(xs),
-        [IN_HBM] * len(xs),
+        [jax.ShapeDtypeStruct((tok, dim), F32)] * parts,
+        [IN_HBM] * parts,
         weight_scratch(w1, w2)
         + [pltpu.VMEM((EXPERTS, most, dim), BF)] * 2
-        + [pltpu.VMEM((ROWS, width), BF), pltpu.VMEM((len(xs), tok, dim), F32)]
-        + [pltpu.SemaphoreType.DMA((EXPERTS, 3)), pltpu.SemaphoreType.DMA((len(xs),))],
+        + [pltpu.VMEM((ROWS, width), BF), pltpu.VMEM((parts, tok, dim), F32)]
+        + [pltpu.SemaphoreType.DMA((EXPERTS, 3)), pltpu.SemaphoreType.DMA((parts,))],
         2 * 3 * tokens * dim * width,
     )
 
 
 def run_dx(xs, gs, maps, w1, w3, w2):
-    tok, dim = xs[0].shape
-    tokens = tok * len(xs)
+    tok, dim = gs[0].shape
+    tokens = tok * len(gs)
     width = w1.shape[2]
     most = tokens + TOKS + ALIGN + ROWS
     kept = 3 * width + 2 * dim
     out = call(
-        dx_kernel, (maps[0], *xs, *gs, maps[1], maps[2], w1, w3, w2),
-        [IN_SMEM] + [IN_VMEM] * 10 + [IN_HBM] * 3,
+        functools.partial(dx_kernel, len(xs)), (maps[0], *xs, *gs, maps[1], maps[2], w1, w3, w2),
+        [IN_SMEM] + [IN_VMEM] * (len(xs) + 6) + [IN_HBM] * 3,
         [jax.ShapeDtypeStruct((tok + 8, dim), F32)] * 4 + [jax.ShapeDtypeStruct((EXPERTS, tokens, kept), BF)],
         [IN_HBM] * 5,
         weight_scratch(w1, w2)
@@ -549,18 +544,28 @@
         dy_own, x_other = lax.optimization_barrier((dy_out, x_all[0]))
         x_all = (x_other, *x_all[1:])
         dy_all = gather(dy_own)
-        far_parts = run_forward(x_all[:2], maps_far, w1_a, w3_a, w2_a)
-        near_parts = run_forward(x_all[2:], maps_near, w1_a, w3_a, w2_a)
-        x_mid = add(x_in, combine((*far_parts, *near_parts)))
-        mid_all = gather(x_mid)
-        x_again, mid_other = lax.optimization_barrier((x_in, mid_all[0]))
-        mid_all = (mid_other, *mid_all[1:])
+        other, diagonal = run_forward(tok, x_all[:2], maps_far, w1_a, w3_a, w2_a)
+        own, mate = run_forward(tok, x_all[2:], maps_near, w1_a, w3_a, w2_a)
+        diagonal = permute(diagonal, beside)
+        mate = permute(mate, beside)
+        half = tok // 2
+        pieces = []
+        for i in range(2):
+            rows = slice(i * half, (i + 1) * half)
+            theirs = permute(other[rows] + diagonal[rows], across)
+            if pieces:
+                theirs, _ = lax.optimization_barrier((theirs, pieces[0]))
+            pieces.append((x_in[rows].astype(F32) + own[rows] + mate[rows] + theirs).astype(BF))
+        gathered = [gather(piece) for piece in pieces]
+        mid_all = [part for pair in zip(*gathered) for part in pair]
+        x_mid = jnp.concatenate(pieces)
+        x_again, mid_all[1] = lax.optimization_barrier((x_in, mid_all[1]))
         again_all = gather_direct(x_again)
         dx_parts, kept_b = run_dx(mid_all, dy_all, maps_b, w1_b, w3_b, w2_b)
         total = combine(dx_parts)
         dx_mid, dgate_b = add(dy_out, total), dgate_of(total)
         dmid_all = gather_direct(dx_mid)
-        x_out = add(x_mid, combine(run_forward(mid_all, maps_b, w1_b, w3_b, w2_b)))
+        x_out = add(x_mid, combine(run_forward(tok, mid_all, maps_b, w1_b, w3_b, w2_b)))
         grads_b = run_dw(kept_b, maps_b, w1_b.shape, w2_b.shape)
         dx_parts, kept_a = run_dx(again_all, dmid_all, maps_a, w1_a, w3_a, w2_a)
         total = combine(dx_parts)

time: 328 us -> 329 us (level)
    ppermute x24 -> x28, waiting for transfers between devices: 93.4 us -> 90.8 us  [permute(): return lax.ppermute(v, 'ep', pairs)]
    add x4 -> x3, other arithmetic: 7.91 us -> 6.04 us  [combine(): theirs = other + permute(diagonal, beside)]
    ppermute x24 -> x28, starting transfers between devices: 78.8 us -> 80.5 us  [permute(): return lax.ppermute(v, 'ep', pairs)]
  transfers between devices with their start and end apart: 24 -> 28, of which waited for: 10 -> 12; matrix products, arithmetic and copies ran while one was open for 5% -> 6% of each run, Pallas kernels for 23% -> 23%
where the time goes in v1:
time: 329 us; the launch traced here: 328 us
  Pallas kernels  129 us (39%)
  waiting for transfers between devices  90.8 us (28%)
  starting transfers between devices  80.5 us (24%)
  other arithmetic  23.1 us (7%)
  local copies, waits for them, and re-layouts  4.21 us (1%)
    pallas_call x7, Pallas kernels, call(): pl.pallas_call(kernel, in_specs=in_specs, out_specs=out_specs, out_shape=...  109 us
    ppermute x28, waiting for transfers between devices, permute(): return lax.ppermute(v, 'ep', pairs)  90.8 us
    ppermute x28, starting transfers between devices, permute(): return lax.ppermute(v, 'ep', pairs)  80.5 us
    pallas_call x1, Pallas kernels, run_gather(): pl.pallas_call(gather_kernel, in_specs=[IN_VMEM] * 2, out_specs=[IN_HBM]...  19.5 us
  transfers between devices with their start and end apart: 28, of which 12 were waited for; matrix products, arithmetic and copies ran while one was open for 6% of the time, Pallas kernels for 23%

profile of v1, /device:TPU:0, one launch (start us, length us, event | category | flops | bytes accessed | tf_op | source)
XLA Modules:
  0.0 328.2 jit_solution(2347656571618501075)
XLA Ops:
  3.3 19.5 %gather_slots.1 = (bf16[512,512]{1,0:T(8,128)(2,1)}, bf16[512,512]{1,0:T(8,128)(2,1)}, bf16[512,512]{1,0:T(8,128)(2,1)}, s32[2,128]{1,0:T(2,128)}, f32[2,2048]{1...) custom-call(f32[8,512]{1,0:T(8,128)} %maximum_bitcast_fusion.map_ref, ...), custom_call_target="tpu_custom_call" | custom-call | flops 10000000 | bytes 4000000 | tf_op jit(solution)/shard_map/gather_slots/pallas_call | solution.py:439
  22.9 9.3 %shard_map.196 = (f32[512,512]{1,0:T(8,128)}, f32[512,512]{1,0:T(8,128)}) custom-call(s32[2,128]{1,0:T(2,128)} %get-tuple-element.60.starts_ref, bf16[512,512]{1,0:T(8,128)(2,1)} %get-tuple-element.62.refs_0_, bf16[512,512]{1,0:T(8,128)(2,1)} %get-tuple-element.63.refs_1_, f32[2,1024]{1,0:T(2,128)} %get-tuple-element.64.refs_2_, ...), custom_call_target="tpu_custom_call" | custom-call | flops 5637144576 | bytes 40000000 | tf_op jit(solution)/shard_map/pallas_call | solution.py:418
  32.8 9.3 %shard_map.195 = (f32[512,512]{1,0:T(8,128)}, f32[512,512]{1,0:T(8,128)}) custom-call(s32[2,128]{1,0:T(2,128)} %get-tuple-element.54.starts_ref, bf16[512,512]{1,0:T(8,128)(2,1)} %refs_2_, bf16[512,512]{1,0:T(8,128)(2,1)} %get-tuple-element.55.refs_1_, f32[2,1024]{1,0:T(2,128)} %get-tuple-element.56.refs_2_, f32[1024,8]{1,0:T(8,128)} %get-tuple-element.57.refs_3_, ...), custom_call_target="tpu_custom_call" | custom-call | flops 5637144576 | bytes 40000000 | tf_op jit(solution)/shard_map/pallas_call | solution.py:418
  42.1 10.3 %collective-permute-start.13 = (bf16[512,512]{1,0:T(8,128)(2,1)}, bf16[512,512]{1,0:T(8,128)(2,1)S(1)}, u32[]{:S(2)}, u32[]{:S(2)}) collective-permute-start(bf16[512,512]{1,0:T(8,128)(2,1)} %refs_10_.3), channel_id=1, source_target_pairs={{0,2},{2,0},{1,3},{3,1},{4,6},{6,4},{5,7},{7,5}} | collective-permute-start | bytes 1572872 | tf_op jit(solution)/shard_map/ppermute | solution.py:519
  52.4 1.8 slice_add_fusion.2
  54.3 2.0 collective-permute-start.3
  56.3 9.1 %collective-permute-done.13.refs_8_ = bf16[512,512]{1,0:T(8,128)(2,1)S(1)} collective-permute-done((bf16[512,512]{1,0:T(8,128)(2,1)}, bf16[512,512]{1,0:T(8,128)(2,1)S(1)}, u32[]{:S(2)}, u32[]{:S(2)}) %collective-permute-start.13) | collective-permute-done | bytes 524320 | tf_op jit(solution)/shard_map/ppermute | solution.py:519
  65.4 11.2 %collective-permute-done.2 = f32[256,512]{1,0:T(8,128)S(1)} collective-permute-done((f32[256,512]{1,0:T(8,128)S(1)}, f32[256,512]{1,0:T(8,128)S(1)}, u32[]{:S(2)}, u32[]{:S(2)}) %collective-permute-start.2) | collective-permute-done | bytes 524320 | tf_op jit(solution)/shard_map/ppermute | solution.py:519
  77.8 9.9 %collective-permute-done.3 = f32[256,512]{1,0:T(8,128)S(1)} collective-permute-done((f32[256,512]{1,0:T(8,128)S(1)}, f32[256,512]{1,0:T(8,128)S(1)}, u32[]{:S(2)}, u32[]{:S(2)}) %collective-permute-start.3) | collective-permute-done | bytes 524320 | tf_op jit(solution)/shard_map/ppermute | solution.py:519
  88.8 1.8 collective-permute-start.5
  91.4 6.6 %collective-permute-done.5.refs_1_ = bf16[256,512]{1,0:T(8,128)(2,1)S(1)} collective-permute-done((bf16[256,512]{1,0:T(8,128)(2,1)S(1)}, bf16[256,512]{1,0:T(8,128)(2,1)S(1)}, u32[]{:S(2)}, u32[]{:S(2)}) %collective-permute-start.5) | collective-permute-done | bytes 262176 | tf_op jit(solution)/shard_map/ppermute | solution.py:519
  98.0 4.5 %collective-permute-done.4.refs_0_ = bf16[256,512]{1,0:T(8,128)(2,1)S(1)} collective-permute-done((bf16[256,512]{1,0:T(8,128)(2,1)S(1)}, bf16[256,512]{1,0:T(8,128)(2,1)S(1)}, u32[]{:S(2)}, u32[]{:S(2)}) %collective-permute-start.4) | collective-permute-done | bytes 262176 | tf_op jit(solution)/shard_map/ppermute | solution.py:519
  104.8 24.1 %shard_map.198 = (f32[520,512]{1,0:T(8,128)}, f32[520,512]{1,0:T(8,128)}, f32[520,512]{1,0:T(8,128)}, f32[520,512]{1,0:T(8,128)}, bf16[2,2048,6400]{2,1,0:T(8,128)(2,1)}) custom-call(s32[2,128]{1,0:T(2,128)} %get-tuple-element.69.starts_ref, bf16[256,512]{1,0:T(8,128)(2,1)} %copy-done.20, bf16[256,512]{1,0:T(8,128)(2,1)} %copy-done.19, ...), custom_call_target="tpu_custom_call" | custom-call | flops 22548578304 | bytes 40000000 | tf_op jit(solution)/shard_map/pallas_call | solution.py:418
  129.4 2.4 collective-permute-done.17
  131.8 2.4 add.73
  134.2 20.2 %collective-permute-start.18 = (f32[520,512]{1,0:T(8,128)}, f32[520,512]{1,0:T(8,128)}, u32[]{:S(2)}, u32[]{:S(2)}) collective-permute-start(f32[520,512]{1,0:T(8,128)} %add.73), channel_id=1, source_target_pairs={{0,2},{2,0},{1,3},{3,1},{4,6},{6,4},{5,7},{7,5}} | collective-permute-start | bytes 3194888 | tf_op jit(solution)/shard_map/ppermute | solution.py:519
  154.5 14.0 %shard_map.197 = (f32[512,512]{1,0:T(8,128)}, f32[512,512]{1,0:T(8,128)}, f32[512,512]{1,0:T(8,128)}, f32[512,512]{1,0:T(8,128)}) custom-call(s32[2,128]{1,0:T(2,128)} %get-tuple-element.69.starts_ref, bf16[256,512]{1,0:T(8,128)(2,1)} %copy-done.20, bf16[256,512]{1,0:T(8,128)(2,1)} %copy-done.19, bf16[256,512]{1,0:T(8,128)(2,1)} %copy-done.24, ...), custom_call_target="tpu_custom_call" | custom-call | flops 11274289152 | bytes 40000000 | tf_op jit(solution)/shard_map/pallas_call | solution.py:418
  169.1 9.2 %collective-permute-start.20 = (bf16[512,512]{1,0:T(8,128)(2,1)}, bf16[512,512]{1,0:T(8,128)(2,1)S(1)}, u32[]{:S(2)}, u32[]{:S(2)}) collective-permute-start(bf16[512,512]{1,0:T(8,128)(2,1)} %refs_2_), channel_id=1, source_target_pairs={{0,3},{3,0},{1,2},{2,1},{4,7},{7,4},{5,6},{6,5}} | collective-permute-start | bytes 1572872 | tf_op jit(solution)/shard_map/ppermute | solution.py:519
  178.7 2.2 add_add_fusion.1
  182.7 1.7 collective-permute-start.23
  185.9 5.0 %collective-permute-done.20.refs_1_ = bf16[512,512]{1,0:T(8,128)(2,1)S(1)} collective-permute-done((bf16[512,512]{1,0:T(8,128)(2,1)}, bf16[512,512]{1,0:T(8,128)(2,1)S(1)}, u32[]{:S(2)}, u32[]{:S(2)}) %collective-permute-start.20) | collective-permute-done | bytes 524320 | tf_op jit(solution)/shard_map/ppermute | solution.py:519
  191.5 11.4 %collective-permute-done.19.refs_0_ = bf16[512,512]{1,0:T(8,128)(2,1)S(1)} collective-permute-done((bf16[512,512]{1,0:T(8,128)(2,1)}, bf16[512,512]{1,0:T(8,128)(2,1)S(1)}, u32[]{:S(2)}, u32[]{:S(2)}) %collective-permute-start.19) | collective-permute-done | bytes 524320 | tf_op jit(solution)/shard_map/ppermute | solution.py:519
  204.5 8.7 %collective-permute-done.23.refs_5_ = bf16[512,512]{1,0:T(8,128)(2,1)S(1)} collective-permute-done((bf16[512,512]{1,0:T(8,128)(2,1)S(1)}, bf16[512,512]{1,0:T(8,128)(2,1)S(1)}, u32[]{:S(2)}, u32[]{:S(2)}) %collective-permute-start.23) | collective-permute-done | bytes 524320 | tf_op jit(solution)/shard_map/ppermute | solution.py:519
  213.3 12.1 %collective-permute-done.22.refs_4_ = bf16[512,512]{1,0:T(8,128)(2,1)S(1)} collective-permute-done((bf16[512,512]{1,0:T(8,128)(2,1)S(1)}, bf16[512,512]{1,0:T(8,128)(2,1)S(1)}, u32[]{:S(2)}, u32[]{:S(2)}) %collective-permute-start.22) | collective-permute-done | bytes 524320 | tf_op jit(solution)/shard_map/ppermute | solution.py:519
  226.1 24.1 %shard_map.199 = (f32[520,512]{1,0:T(8,128)}, f32[520,512]{1,0:T(8,128)}, f32[520,512]{1,0:T(8,128)}, f32[520,512]{1,0:T(8,128)}, bf16[2,2048,6400]{2,1,0:T(8,128)(2,1)}) custom-call(s32[2,128]{1,0:T(2,128)} %get-tuple-element.82.starts_ref, bf16[512,512]{1,0:T(8,128)(2,1)} %copy-done.15, bf16[512,512]{1,0:T(8,128)(2,1)} %copy-done.14, ...), custom_call_target="tpu_custom_call" | custom-call | flops 22548578304 | bytes 40000000 | tf_op jit(solution)/shard_map/pallas_call | solution.py:418
  250.3 14.2 %shard_map.201 = (f32[2,512,1792]{2,1,0:T(8,128)}, f32[2,512,1792]{2,1,0:T(8,128)}, f32[2,1792,512]{2,1,0:T(8,128)}) custom-call(s32[2,128]{1,0:T(2,128)} %get-tuple-element.69.starts_ref, bf16[2,2048,6400]{2,1,0:T(8,128)(2,1)} %get-tuple-element.94.kept_hbm), custom_call_target="tpu_custom_call" | custom-call | flops 11274289152 | bytes 40000000 | tf_op jit(solution)/shard_map/pallas_call | solution.py:418
  264.6 3.2 add_convert_fusion
  268.2 2.4 add.77
  270.7 29.2 %collective-permute-start.27 = (f32[520,512]{1,0:T(8,128)}, f32[520,512]{1,0:T(8,128)}, u32[]{:S(2)}, u32[]{:S(2)}) collective-permute-start(f32[520,512]{1,0:T(8,128)} %add.77), channel_id=1, source_target_pairs={{0,2},{2,0},{1,3},{3,1},{4,6},{6,4},{5,7},{7,5}} | collective-permute-start | bytes 3194888 | tf_op jit(solution)/shard_map/ppermute | solution.py:519
  301.2 14.0 %shard_map.200 = (f32[2,512,1792]{2,1,0:T(8,128)}, f32[2,512,1792]{2,1,0:T(8,128)}, f32[2,1792,512]{2,1,0:T(8,128)}) custom-call(s32[2,128]{1,0:T(2,128)} %get-tuple-element.82.starts_ref, bf16[2,2048,6400]{2,1,0:T(8,128)(2,1)} %get-tuple-element.90.kept_hbm), custom_call_target="tpu_custom_call" | custom-call | flops 11274289152 | bytes 40000000 | tf_op jit(solution)/shard_map/pallas_call | solution.py:418
  315.2 9.1 %collective-permute-done.27 = f32[520,512]{1,0:T(8,128)} collective-permute-done((f32[520,512]{1,0:T(8,128)}, f32[520,512]{1,0:T(8,128)}, u32[]{:S(2)}, u32[]{:S(2)}) %collective-permute-start.27) | collective-permute-done | bytes 1064992 | tf_op jit(solution)/shard_map/ppermute | solution.py:519
  324.4 2.3 add_add_fusion
  (98 shorter events, 19.8 us)
Async XLA Ops:
  32.2 20.2 %collective-permute-start.1 = (f32[512,512]{1,0:T(8,128)}, f32[512,512]{1,0:T(8,128)}, u32[]{:S(2)}, u32[]{:S(2)}) collective-permute-start(f32[512,512]{1,0:T(8,128)} %get-tuple-element.67), channel_id=1, source_target_pairs={{0,1},{1,0},{2,3},{3,2},{4,5},{5,4},{6,7},{7,6}} | collective-permute-start | bytes 3145736 | tf_op jit(solution)/shard_map/ppermute | solution.py:519
  42.1 23.3 %collective-permute-start = (f32[512,512]{1,0:T(8,128)}, f32[512,512]{1,0:T(8,128)S(1)}, u32[]{:S(2)}, u32[]{:S(2)}) collective-permute-start(f32[512,512]{1,0:T(8,128)} %get-tuple-element.59), channel_id=1, source_target_pairs={{0,1},{1,0},{2,3},{3,2},{4,5},{5,4},{6,7},{7,6}} | collective-permute-start | bytes 3145736 | tf_op jit(solution)/shard_map/ppermute | solution.py:519
  42.1 23.3 %collective-permute-start.13 = (bf16[512,512]{1,0:T(8,128)(2,1)}, bf16[512,512]{1,0:T(8,128)(2,1)S(1)}, u32[]{:S(2)}, u32[]{:S(2)}) collective-permute-start(bf16[512,512]{1,0:T(8,128)(2,1)} %refs_10_.3), channel_id=1, source_target_pairs={{0,2},{2,0},{1,3},{3,1},{4,6},{6,4},{5,7},{7,5}} | collective-permute-start | bytes 1572872 | tf_op jit(solution)/shard_map/ppermute | solution.py:519
  52.4 24.2 %copy-start.5 = (f32[512,512]{1,0:T(8,128)S(1)}, f32[512,512]{1,0:T(8,128)}, u32[]{:S(2)}) copy-start(f32[512,512]{1,0:T(8,128)} %get-tuple-element.58) | copy-start | bytes 3145732
  54.2 22.4 %collective-permute-start.2 = (f32[256,512]{1,0:T(8,128)S(1)}, f32[256,512]{1,0:T(8,128)S(1)}, u32[]{:S(2)}, u32[]{:S(2)}) collective-permute-start(f32[256,512]{1,0:T(8,128)S(1)} %get-tuple-element.99), channel_id=1, source_target_pairs={{0,2},{2,0},{1,3},{3,1},{4,6},{6,4},{5,7},{7,5}} | collective-permute-start | bytes 1572872 | tf_op jit(solution)/shard_map/ppermute | solution.py:519
  54.3 33.4 %collective-permute-start.3 = (f32[256,512]{1,0:T(8,128)S(1)}, f32[256,512]{1,0:T(8,128)S(1)}, u32[]{:S(2)}, u32[]{:S(2)}) collective-permute-start(f32[256,512]{1,0:T(8,128)S(1)} %get-tuple-element.98), channel_id=1, source_target_pairs={{0,2},{2,0},{1,3},{3,1},{4,6},{6,4},{5,7},{7,5}} | collective-permute-start | bytes 1572872 | tf_op jit(solution)/shard_map/ppermute | solution.py:519
  56.3 34.6 %collective-permute-start.15 = (bf16[512,512]{1,0:T(8,128)(2,1)}, bf16[512,512]{1,0:T(8,128)(2,1)S(1)}, u32[]{:S(2)}, u32[]{:S(2)}) collective-permute-start(bf16[512,512]{1,0:T(8,128)(2,1)} %refs_10_.3), channel_id=1, source_target_pairs={{0,1},{1,0},{2,3},{3,2},{4,5},{5,4},{6,7},{7,6}} | collective-permute-start | bytes 1572872 | tf_op jit(solution)/shard_map/ppermute | solution.py:519
  65.4 23.4 %copy-start.10 = (bf16[512,512]{1,0:T(8,128)(2,1)}, bf16[512,512]{1,0:T(8,128)(2,1)S(1)}, u32[]{:S(2)}) copy-start(bf16[512,512]{1,0:T(8,128)(2,1)S(1)} %collective-permute-done.13.refs_8_) | copy-start | bytes 1572868
  65.4 37.2 %collective-permute-start.14 = (bf16[512,512]{1,0:T(8,128)(2,1)S(1)}, bf16[512,512]{1,0:T(8,128)(2,1)S(1)}, u32[]{:S(2)}, u32[]{:S(2)}) collective-permute-start(bf16[512,512]{1,0:T(8,128)(2,1)S(1)} %collective-permute-done.13.refs_8_), channel_id=1, source_target_pairs={{0,1},{1,0},{2,3},{3,2},{4,5},{5,4},{6,7},{7,6}} | collective-permute-start | bytes 1572872 | tf_op jit(solution)/shard_map/ppermute | solution.py:519
  77.7 27.0 %copy-start.6 = (bf16[256,512]{1,0:T(8,128)(2,1)}, bf16[256,512]{1,0:T(8,128)(2,1)S(1)}, u32[]{:S(2)}) copy-start(bf16[256,512]{1,0:T(8,128)(2,1)S(1)} %fusion.5.refs_4_) | copy-start | bytes 786436
  88.8 9.2 %collective-permute-start.5 = (bf16[256,512]{1,0:T(8,128)(2,1)S(1)}, bf16[256,512]{1,0:T(8,128)(2,1)S(1)}, u32[]{:S(2)}, u32[]{:S(2)}) collective-permute-start(bf16[256,512]{1,0:T(8,128)(2,1)S(1)} %fusion.3.refs_5_), channel_id=1, source_target_pairs={{0,2},{2,0},{1,3},{3,1},{4,6},{6,4},{5,7},{7,5}} | collective-permute-start | bytes 786440 | tf_op jit(solution)/shard_map/ppermute | solution.py:519
  90.6 12.0 %collective-permute-start.4 = (bf16[256,512]{1,0:T(8,128)(2,1)S(1)}, bf16[256,512]{1,0:T(8,128)(2,1)S(1)}, u32[]{:S(2)}, u32[]{:S(2)}) collective-permute-start(bf16[256,512]{1,0:T(8,128)(2,1)S(1)} %fusion.5.refs_4_), channel_id=1, source_target_pairs={{0,2},{2,0},{1,3},{3,1},{4,6},{6,4},{5,7},{7,5}} | collective-permute-start | bytes 786440 | tf_op jit(solution)/shard_map/ppermute | solution.py:519
  90.8 11.7 %collective-permute-start.9 = (bf16[256,512]{1,0:T(8,128)(2,1)S(1)}, bf16[256,512]{1,0:T(8,128)(2,1)S(1)}, u32[]{:S(2)}, u32[]{:S(2)}) collective-permute-start(bf16[256,512]{1,0:T(8,128)(2,1)S(1)} %fusion.3.refs_5_), channel_id=1, source_target_pairs={{0,1},{1,0},{2,3},{3,2},{4,5},{5,4},{6,7},{7,6}} | collective-permute-start | bytes 786440 | tf_op jit(solution)/shard_map/ppermute | solution.py:519
  90.8 11.7 %collective-permute-start.8 = (bf16[256,512]{1,0:T(8,128)(2,1)S(1)}, bf16[256,512]{1,0:T(8,128)(2,1)S(1)}, u32[]{:S(2)}, u32[]{:S(2)}) collective-permute-start(bf16[256,512]{1,0:T(8,128)(2,1)S(1)} %fusion.5.refs_4_), channel_id=1, source_target_pairs={{0,1},{1,0},{2,3},{3,2},{4,5},{5,4},{6,7},{7,6}} | collective-permute-start | bytes 786440 | tf_op jit(solution)/shard_map/ppermute | solution.py:519
  98.0 4.6 %collective-permute-start.7 = (bf16[256,512]{1,0:T(8,128)(2,1)S(1)}, bf16[256,512]{1,0:T(8,128)(2,1)S(1)}, u32[]{:S(2)}, u32[]{:S(2)}) collective-permute-start(bf16[256,512]{1,0:T(8,128)(2,1)S(1)} %collective-permute-done.5.refs_1_), channel_id=1, source_target_pairs={{0,1},{1,0},{2,3},{3,2},{4,5},{5,4},{6,7},{7,6}} | collective-permute-start | bytes 786440 | tf_op jit(solution)/shard_map/ppermute | solution.py:519
  102.5 1.5 collective-permute-start.6
  128.9 2.9 collective-permute-start.17
  129.1 49.2 %collective-permute-start.16 = (f32[520,512]{1,0:T(8,128)}, f32[520,512]{1,0:T(8,128)}, u32[]{:S(2)}, u32[]{:S(2)}) collective-permute-start(f32[520,512]{1,0:T(8,128)} %get-tuple-element.79), channel_id=1, source_target_pairs={{0,1},{1,0},{2,3},{3,2},{4,5},{5,4},{6,7},{7,6}} | collective-permute-start | bytes 3194888 | tf_op jit(solution)/shard_map/ppermute | solution.py:519
  134.2 44.4 %collective-permute-start.18 = (f32[520,512]{1,0:T(8,128)}, f32[520,512]{1,0:T(8,128)}, u32[]{:S(2)}, u32[]{:S(2)}) collective-permute-start(f32[520,512]{1,0:T(8,128)} %add.73), channel_id=1, source_target_pairs={{0,2},{2,0},{1,3},{3,1},{4,6},{6,4},{5,7},{7,5}} | collective-permute-start | bytes 3194888 | tf_op jit(solution)/shard_map/ppermute | solution.py:519
  168.5 15.9 %collective-permute-start.11 = (f32[512,512]{1,0:T(8,128)}, f32[512,512]{1,0:T(8,128)S(1)}, u32[]{:S(2)}, u32[]{:S(2)}) collective-permute-start(f32[512,512]{1,0:T(8,128)} %get-tuple-element.76), channel_id=1, source_target_pairs={{0,1},{1,0},{2,3},{3,2},{4,5},{5,4},{6,7},{7,6}} | collective-permute-start | bytes 3145736 | tf_op jit(solution)/shard_map/ppermute | solution.py:519
  168.6 14.1 %collective-permute-start.21 = (bf16[512,512]{1,0:T(8,128)(2,1)}, bf16[512,512]{1,0:T(8,128)(2,1)S(1)}, u32[]{:S(2)}, u32[]{:S(2)}) collective-permute-start(bf16[512,512]{1,0:T(8,128)(2,1)} %refs_2_), channel_id=1, source_target_pairs={{0,1},{1,0},{2,3},{3,2},{4,5},{5,4},{6,7},{7,6}} | collective-permute-start | bytes 1572872 | tf_op jit(solution)/shard_map/ppermute | solution.py:519
  169.1 21.8 %collective-permute-start.20 = (bf16[512,512]{1,0:T(8,128)(2,1)}, bf16[512,512]{1,0:T(8,128)(2,1)S(1)}, u32[]{:S(2)}, u32[]{:S(2)}) collective-permute-start(bf16[512,512]{1,0:T(8,128)(2,1)} %refs_2_), channel_id=1, source_target_pairs={{0,3},{3,0},{1,2},{2,1},{4,7},{7,4},{5,6},{6,5}} | collective-permute-start | bytes 1572872 | tf_op jit(solution)/shard_map/ppermute | solution.py:519
  178.3 24.6 %collective-permute-start.19 = (bf16[512,512]{1,0:T(8,128)(2,1)}, bf16[512,512]{1,0:T(8,128)(2,1)S(1)}, u32[]{:S(2)}, u32[]{:S(2)}) collective-permute-start(bf16[512,512]{1,0:T(8,128)(2,1)} %refs_2_), channel_id=1, source_target_pairs={{0,2},{2,0},{1,3},{3,1},{4,6},{6,4},{5,7},{7,5}} | collective-permute-start | bytes 1572872 | tf_op jit(solution)/shard_map/ppermute | solution.py:519
  182.6 22.0 %collective-permute-start.24 = (bf16[512,512]{1,0:T(8,128)(2,1)S(1)}, bf16[512,512]{1,0:T(8,128)(2,1)S(1)}, u32[]{:S(2)}, u32[]{:S(2)}) collective-permute-start(bf16[512,512]{1,0:T(8,128)(2,1)S(1)} %fusion.1.refs_6_), channel_id=1, source_target_pairs={{0,1},{1,0},{2,3},{3,2},{4,5},{5,4},{6,7},{7,6}} | collective-permute-start | bytes 1572872 | tf_op jit(solution)/shard_map/ppermute | solution.py:519
  182.7 30.6 %collective-permute-start.23 = (bf16[512,512]{1,0:T(8,128)(2,1)S(1)}, bf16[512,512]{1,0:T(8,128)(2,1)S(1)}, u32[]{:S(2)}, u32[]{:S(2)}) collective-permute-start(bf16[512,512]{1,0:T(8,128)(2,1)S(1)} %fusion.1.refs_6_), channel_id=1, source_target_pairs={{0,3},{3,0},{1,2},{2,1},{4,7},{7,4},{5,6},{6,5}} | collective-permute-start | bytes 1572872 | tf_op jit(solution)/shard_map/ppermute | solution.py:519
  184.4 40.9 %collective-permute-start.22 = (bf16[512,512]{1,0:T(8,128)(2,1)S(1)}, bf16[512,512]{1,0:T(8,128)(2,1)S(1)}, u32[]{:S(2)}, u32[]{:S(2)}) collective-permute-start(bf16[512,512]{1,0:T(8,128)(2,1)S(1)} %fusion.1.refs_6_), channel_id=1, source_target_pairs={{0,2},{2,0},{1,3},{3,1},{4,6},{6,4},{5,7},{7,5}} | collective-permute-start | bytes 1572872 | tf_op jit(solution)/shard_map/ppermute | solution.py:519
  190.9 34.4 %copy-start.14 = (bf16[512,512]{1,0:T(8,128)(2,1)}, bf16[512,512]{1,0:T(8,128)(2,1)S(1)}, u32[]{:S(2)}) copy-start(bf16[512,512]{1,0:T(8,128)(2,1)S(1)} %collective-permute-done.20.refs_1_) | copy-start | bytes 1572868
  190.9 73.6 %collective-permute-start.10 = (f32[512,512]{1,0:T(8,128)}, f32[512,512]{1,0:T(8,128)}, u32[]{:S(2)}, u32[]{:S(2)}) collective-permute-start(f32[512,512]{1,0:T(8,128)} %get-tuple-element.74), channel_id=1, source_target_pairs={{0,1},{1,0},{2,3},{3,2},{4,5},{5,4},{6,7},{7,6}} | collective-permute-start | bytes 3145736 | tf_op jit(solution)/shard_map/ppermute | solution.py:519
  202.9 61.7 %collective-permute-start.12 = (f32[512,512]{1,0:T(8,128)}, f32[512,512]{1,0:T(8,128)}, u32[]{:S(2)}, u32[]{:S(2)}) collective-permute-start(f32[512,512]{1,0:T(8,128)} %add.69), channel_id=1, source_target_pairs={{0,2},{2,0},{1,3},{3,1},{4,6},{6,4},{5,7},{7,5}} | collective-permute-start | bytes 3145736 | tf_op jit(solution)/shard_map/ppermute | solution.py:519
  250.3 17.9 %collective-permute-start.26 = (f32[520,512]{1,0:T(8,128)}, f32[520,512]{1,0:T(8,128)}, u32[]{:S(2)}, u32[]{:S(2)}) collective-permute-start(f32[520,512]{1,0:T(8,128)} %get-tuple-element.89), channel_id=1, source_target_pairs={{0,1},{1,0},{2,3},{3,2},{4,5},{5,4},{6,7},{7,6}} | collective-permute-start | bytes 3194888 | tf_op jit(solution)/shard_map/ppermute | solution.py:519
  267.8 47.5 %collective-permute-start.25 = (f32[520,512]{1,0:T(8,128)}, f32[520,512]{1,0:T(8,128)}, u32[]{:S(2)}, u32[]{:S(2)}) collective-permute-start(f32[520,512]{1,0:T(8,128)} %get-tuple-element.87), channel_id=1, source_target_pairs={{0,1},{1,0},{2,3},{3,2},{4,5},{5,4},{6,7},{7,6}} | collective-permute-start | bytes 3194888 | tf_op jit(solution)/shard_map/ppermute | solution.py:519
  270.7 53.7 %collective-permute-start.27 = (f32[520,512]{1,0:T(8,128)}, f32[520,512]{1,0:T(8,128)}, u32[]{:S(2)}, u32[]{:S(2)}) collective-permute-start(f32[520,512]{1,0:T(8,128)} %add.77), channel_id=1, source_target_pairs={{0,2},{2,0},{1,3},{3,1},{4,6},{6,4},{5,7},{7,5}} | collective-permute-start | bytes 3194888 | tf_op jit(solution)/shard_map/ppermute | solution.py:519
  (21 other events, 147.4 us)

commit v2 on v1

--- a/solution.py
+++ b/solution.py
@@ -429,7 +429,7 @@
 def run_gather(own_map, x):
     tok, dim = x.shape
     tokens = 4 * tok
-    pieces = 4
+    pieces = 8
     outs = []
     for size in (tokens, tokens, tokens // 2, tokens // 2):
         outs.append(jax.ShapeDtypeStruct((EXPERTS, 128), jnp.int32))
@@ -532,7 +532,8 @@
 
     def device_program(x_in, idx_a, idx_b, gate_a, gate_b, dy_out, w1_a, w3_a, w2_a, w1_b, w3_b, w2_b):
         tok, top_k = idx_a.shape
-        own_map = jnp.concatenate([idx_a.astype(F32), idx_b.astype(F32), gate_a, gate_b], axis=1).T
+        ids = jnp.concatenate([idx_a.T, idx_b.T]).astype(F32)
+        own_map = jnp.concatenate([ids, gate_a.T, gate_b.T])
         x_all, (maps_a, maps_b, maps_far, maps_near) = run_gather(own_map, x_in)
 
         def add(base, total):

time: 329 us -> 328 us (level)
  no operation moved by 1% of the time
where the time goes in v2:
time: 328 us
  Pallas kernels  129 us (39%)
  waiting for transfers between devices  90.8 us (28%)
  starting transfers between devices  80.5 us (25%)
  other arithmetic  22.4 us (7%)
  local copies, waits for them, and re-layouts  4.21 us (1%)
    pallas_call x7, Pallas kernels, call(): pl.pallas_call(kernel, in_specs=in_specs, out_specs=out_specs, out_shape=...  109 us
    ppermute x28, waiting for transfers between devices, permute(): return lax.ppermute(v, 'ep', pairs)  90.8 us
    ppermute x28, starting transfers between devices, permute(): return lax.ppermute(v, 'ep', pairs)  80.5 us
    pallas_call x1, Pallas kernels, run_gather(): pl.pallas_call(gather_kernel, in_specs=[IN_VMEM] * 2, out_specs=[IN_HBM]...  19.6 us
  transfers between devices with their start and end apart: 28, of which 12 were waited for; matrix products, arithmetic and copies ran while one was open for 6% of the time, Pallas kernels for 23%

profile of v2, /device:TPU:0, one launch (start us, length us, event | category | flops | bytes accessed | tf_op | source)
XLA Modules:
  0.0 327.6 jit_solution(2430600448603282946)
XLA Ops:
  2.7 19.6 %gather_slots.1 = (bf16[512,512]{1,0:T(8,128)(2,1)}, bf16[512,512]{1,0:T(8,128)(2,1)}, bf16[512,512]{1,0:T(8,128)(2,1)}, s32[2,128]{1,0:T(2,128)}, f32[2,2048]{1...) custom-call(f32[8,512]{1,0:T(8,128)} %pad_maximum_fusion.map_ref, ...), custom_call_target="tpu_custom_call" | custom-call | flops 10000000 | bytes 4000000 | tf_op jit(solution)/shard_map/gather_slots/pallas_call | solution.py:439
  22.2 9.3 %shard_map.196 = (f32[512,512]{1,0:T(8,128)}, f32[512,512]{1,0:T(8,128)}) custom-call(s32[2,128]{1,0:T(2,128)} %get-tuple-element.60.starts_ref, bf16[512,512]{1,0:T(8,128)(2,1)} %get-tuple-element.62.refs_0_, bf16[512,512]{1,0:T(8,128)(2,1)} %get-tuple-element.63.refs_1_, f32[2,1024]{1,0:T(2,128)} %get-tuple-element.64.refs_2_, ...), custom_call_target="tpu_custom_call" | custom-call | flops 5637144576 | bytes 40000000 | tf_op jit(solution)/shard_map/pallas_call | solution.py:418
  32.2 9.3 %shard_map.195 = (f32[512,512]{1,0:T(8,128)}, f32[512,512]{1,0:T(8,128)}) custom-call(s32[2,128]{1,0:T(2,128)} %get-tuple-element.54.starts_ref, bf16[512,512]{1,0:T(8,128)(2,1)} %refs_2_, bf16[512,512]{1,0:T(8,128)(2,1)} %get-tuple-element.55.refs_1_, f32[2,1024]{1,0:T(2,128)} %get-tuple-element.56.refs_2_, f32[1024,8]{1,0:T(8,128)} %get-tuple-element.57.refs_3_, ...), custom_call_target="tpu_custom_call" | custom-call | flops 5637144576 | bytes 40000000 | tf_op jit(solution)/shard_map/pallas_call | solution.py:418
  41.5 10.3 %collective-permute-start.13 = (bf16[512,512]{1,0:T(8,128)(2,1)}, bf16[512,512]{1,0:T(8,128)(2,1)S(1)}, u32[]{:S(2)}, u32[]{:S(2)}) collective-permute-start(bf16[512,512]{1,0:T(8,128)(2,1)} %refs_10_.3), channel_id=1, source_target_pairs={{0,2},{2,0},{1,3},{3,1},{4,6},{6,4},{5,7},{7,5}} | collective-permute-start | bytes 1572872 | tf_op jit(solution)/shard_map/ppermute | solution.py:519
  51.8 1.8 slice_add_fusion.2
  53.7 2.0 collective-permute-start.3
  55.7 9.1 %collective-permute-done.13.refs_8_ = bf16[512,512]{1,0:T(8,128)(2,1)S(1)} collective-permute-done((bf16[512,512]{1,0:T(8,128)(2,1)}, bf16[512,512]{1,0:T(8,128)(2,1)S(1)}, u32[]{:S(2)}, u32[]{:S(2)}) %collective-permute-start.13) | collective-permute-done | bytes 524320 | tf_op jit(solution)/shard_map/ppermute | solution.py:519
  64.8 11.2 %collective-permute-done.2 = f32[256,512]{1,0:T(8,128)S(1)} collective-permute-done((f32[256,512]{1,0:T(8,128)S(1)}, f32[256,512]{1,0:T(8,128)S(1)}, u32[]{:S(2)}, u32[]{:S(2)}) %collective-permute-start.2) | collective-permute-done | bytes 524320 | tf_op jit(solution)/shard_map/ppermute | solution.py:519
  77.2 9.9 %collective-permute-done.3 = f32[256,512]{1,0:T(8,128)S(1)} collective-permute-done((f32[256,512]{1,0:T(8,128)S(1)}, f32[256,512]{1,0:T(8,128)S(1)}, u32[]{:S(2)}, u32[]{:S(2)}) %collective-permute-start.3) | collective-permute-done | bytes 524320 | tf_op jit(solution)/shard_map/ppermute | solution.py:519
  88.2 1.8 collective-permute-start.5
  90.8 6.6 %collective-permute-done.5.refs_1_ = bf16[256,512]{1,0:T(8,128)(2,1)S(1)} collective-permute-done((bf16[256,512]{1,0:T(8,128)(2,1)S(1)}, bf16[256,512]{1,0:T(8,128)(2,1)S(1)}, u32[]{:S(2)}, u32[]{:S(2)}) %collective-permute-start.5) | collective-permute-done | bytes 262176 | tf_op jit(solution)/shard_map/ppermute | solution.py:519
  97.4 4.5 %collective-permute-done.4.refs_0_ = bf16[256,512]{1,0:T(8,128)(2,1)S(1)} collective-permute-done((bf16[256,512]{1,0:T(8,128)(2,1)S(1)}, bf16[256,512]{1,0:T(8,128)(2,1)S(1)}, u32[]{:S(2)}, u32[]{:S(2)}) %collective-permute-start.4) | collective-permute-done | bytes 262176 | tf_op jit(solution)/shard_map/ppermute | solution.py:519
  104.2 24.1 %shard_map.198 = (f32[520,512]{1,0:T(8,128)}, f32[520,512]{1,0:T(8,128)}, f32[520,512]{1,0:T(8,128)}, f32[520,512]{1,0:T(8,128)}, bf16[2,2048,6400]{2,1,0:T(8,128)(2,1)}) custom-call(s32[2,128]{1,0:T(2,128)} %get-tuple-element.69.starts_ref, bf16[256,512]{1,0:T(8,128)(2,1)} %copy-done.20, bf16[256,512]{1,0:T(8,128)(2,1)} %copy-done.19, ...), custom_call_target="tpu_custom_call" | custom-call | flops 22548578304 | bytes 40000000 | tf_op jit(solution)/shard_map/pallas_call | solution.py:418
  128.8 2.4 collective-permute-done.17
  131.2 2.4 add.73
  133.6 20.2 %collective-permute-start.18 = (f32[520,512]{1,0:T(8,128)}, f32[520,512]{1,0:T(8,128)}, u32[]{:S(2)}, u32[]{:S(2)}) collective-permute-start(f32[520,512]{1,0:T(8,128)} %add.73), channel_id=1, source_target_pairs={{0,2},{2,0},{1,3},{3,1},{4,6},{6,4},{5,7},{7,5}} | collective-permute-start | bytes 3194888 | tf_op jit(solution)/shard_map/ppermute | solution.py:519
  153.9 14.0 %shard_map.197 = (f32[512,512]{1,0:T(8,128)}, f32[512,512]{1,0:T(8,128)}, f32[512,512]{1,0:T(8,128)}, f32[512,512]{1,0:T(8,128)}) custom-call(s32[2,128]{1,0:T(2,128)} %get-tuple-element.69.starts_ref, bf16[256,512]{1,0:T(8,128)(2,1)} %copy-done.20, bf16[256,512]{1,0:T(8,128)(2,1)} %copy-done.19, bf16[256,512]{1,0:T(8,128)(2,1)} %copy-done.24, ...), custom_call_target="tpu_custom_call" | custom-call | flops 11274289152 | bytes 40000000 | tf_op jit(solution)/shard_map/pallas_call | solution.py:418
  168.5 9.2 %collective-permute-start.20 = (bf16[512,512]{1,0:T(8,128)(2,1)}, bf16[512,512]{1,0:T(8,128)(2,1)S(1)}, u32[]{:S(2)}, u32[]{:S(2)}) collective-permute-start(bf16[512,512]{1,0:T(8,128)(2,1)} %refs_2_), channel_id=1, source_target_pairs={{0,3},{3,0},{1,2},{2,1},{4,7},{7,4},{5,6},{6,5}} | collective-permute-start | bytes 1572872 | tf_op jit(solution)/shard_map/ppermute | solution.py:519
  178.1 2.2 add_add_fusion.1
  182.1 1.7 collective-permute-start.23
  185.4 5.0 %collective-permute-done.20.refs_1_ = bf16[512,512]{1,0:T(8,128)(2,1)S(1)} collective-permute-done((bf16[512,512]{1,0:T(8,128)(2,1)}, bf16[512,512]{1,0:T(8,128)(2,1)S(1)}, u32[]{:S(2)}, u32[]{:S(2)}) %collective-permute-start.20) | collective-permute-done | bytes 524320 | tf_op jit(solution)/shard_map/ppermute | solution.py:519
  190.9 11.4 %collective-permute-done.19.refs_0_ = bf16[512,512]{1,0:T(8,128)(2,1)S(1)} collective-permute-done((bf16[512,512]{1,0:T(8,128)(2,1)}, bf16[512,512]{1,0:T(8,128)(2,1)S(1)}, u32[]{:S(2)}, u32[]{:S(2)}) %collective-permute-start.19) | collective-permute-done | bytes 524320 | tf_op jit(solution)/shard_map/ppermute | solution.py:519
  203.9 8.7 %collective-permute-done.23.refs_5_ = bf16[512,512]{1,0:T(8,128)(2,1)S(1)} collective-permute-done((bf16[512,512]{1,0:T(8,128)(2,1)S(1)}, bf16[512,512]{1,0:T(8,128)(2,1)S(1)}, u32[]{:S(2)}, u32[]{:S(2)}) %collective-permute-start.23) | collective-permute-done | bytes 524320 | tf_op jit(solution)/shard_map/ppermute | solution.py:519
  212.7 12.1 %collective-permute-done.22.refs_4_ = bf16[512,512]{1,0:T(8,128)(2,1)S(1)} collective-permute-done((bf16[512,512]{1,0:T(8,128)(2,1)S(1)}, bf16[512,512]{1,0:T(8,128)(2,1)S(1)}, u32[]{:S(2)}, u32[]{:S(2)}) %collective-permute-start.22) | collective-permute-done | bytes 524320 | tf_op jit(solution)/shard_map/ppermute | solution.py:519
  225.5 24.1 %shard_map.199 = (f32[520,512]{1,0:T(8,128)}, f32[520,512]{1,0:T(8,128)}, f32[520,512]{1,0:T(8,128)}, f32[520,512]{1,0:T(8,128)}, bf16[2,2048,6400]{2,1,0:T(8,128)(2,1)}) custom-call(s32[2,128]{1,0:T(2,128)} %get-tuple-element.82.starts_ref, bf16[512,512]{1,0:T(8,128)(2,1)} %copy-done.15, bf16[512,512]{1,0:T(8,128)(2,1)} %copy-done.14, ...), custom_call_target="tpu_custom_call" | custom-call | flops 22548578304 | bytes 40000000 | tf_op jit(solution)/shard_map/pallas_call | solution.py:418
  249.8 14.2 %shard_map.201 = (f32[2,512,1792]{2,1,0:T(8,128)}, f32[2,512,1792]{2,1,0:T(8,128)}, f32[2,1792,512]{2,1,0:T(8,128)}) custom-call(s32[2,128]{1,0:T(2,128)} %get-tuple-element.69.starts_ref, bf16[2,2048,6400]{2,1,0:T(8,128)(2,1)} %get-tuple-element.94.kept_hbm), custom_call_target="tpu_custom_call" | custom-call | flops 11274289152 | bytes 40000000 | tf_op jit(solution)/shard_map/pallas_call | solution.py:418
  264.0 3.2 add_convert_fusion
  267.6 2.4 add.77
  270.1 29.2 %collective-permute-start.27 = (f32[520,512]{1,0:T(8,128)}, f32[520,512]{1,0:T(8,128)}, u32[]{:S(2)}, u32[]{:S(2)}) collective-permute-start(f32[520,512]{1,0:T(8,128)} %add.77), channel_id=1, source_target_pairs={{0,2},{2,0},{1,3},{3,1},{4,6},{6,4},{5,7},{7,5}} | collective-permute-start | bytes 3194888 | tf_op jit(solution)/shard_map/ppermute | solution.py:519
  300.6 14.0 %shard_map.200 = (f32[2,512,1792]{2,1,0:T(8,128)}, f32[2,512,1792]{2,1,0:T(8,128)}, f32[2,1792,512]{2,1,0:T(8,128)}) custom-call(s32[2,128]{1,0:T(2,128)} %get-tuple-element.82.starts_ref, bf16[2,2048,6400]{2,1,0:T(8,128)(2,1)} %get-tuple-element.90.kept_hbm), custom_call_target="tpu_custom_call" | custom-call | flops 11274289152 | bytes 40000000 | tf_op jit(solution)/shard_map/pallas_call | solution.py:418
  314.6 9.1 %collective-permute-done.27 = f32[520,512]{1,0:T(8,128)} collective-permute-done((f32[520,512]{1,0:T(8,128)}, f32[520,512]{1,0:T(8,128)}, u32[]{:S(2)}, u32[]{:S(2)}) %collective-permute-start.27) | collective-permute-done | bytes 1064992 | tf_op jit(solution)/shard_map/ppermute | solution.py:519
  323.8 2.3 add_add_fusion
  (97 shorter events, 19.2 us)
Async XLA Ops:
  31.5 20.2 %collective-permute-start.1 = (f32[512,512]{1,0:T(8,128)}, f32[512,512]{1,0:T(8,128)}, u32[]{:S(2)}, u32[]{:S(2)}) collective-permute-start(f32[512,512]{1,0:T(8,128)} %get-tuple-element.67), channel_id=1, source_target_pairs={{0,1},{1,0},{2,3},{3,2},{4,5},{5,4},{6,7},{7,6}} | collective-permute-start | bytes 3145736 | tf_op jit(solution)/shard_map/ppermute | solution.py:519
  41.5 23.3 %collective-permute-start = (f32[512,512]{1,0:T(8,128)}, f32[512,512]{1,0:T(8,128)S(1)}, u32[]{:S(2)}, u32[]{:S(2)}) collective-permute-start(f32[512,512]{1,0:T(8,128)} %get-tuple-element.59), channel_id=1, source_target_pairs={{0,1},{1,0},{2,3},{3,2},{4,5},{5,4},{6,7},{7,6}} | collective-permute-start | bytes 3145736 | tf_op jit(solution)/shard_map/ppermute | solution.py:519
  41.5 23.3 %collective-permute-start.13 = (bf16[512,512]{1,0:T(8,128)(2,1)}, bf16[512,512]{1,0:T(8,128)(2,1)S(1)}, u32[]{:S(2)}, u32[]{:S(2)}) collective-permute-start(bf16[512,512]{1,0:T(8,128)(2,1)} %refs_10_.3), channel_id=1, source_target_pairs={{0,2},{2,0},{1,3},{3,1},{4,6},{6,4},{5,7},{7,5}} | collective-permute-start | bytes 1572872 | tf_op jit(solution)/shard_map/ppermute | solution.py:519
  51.8 24.2 %copy-start.5 = (f32[512,512]{1,0:T(8,128)S(1)}, f32[512,512]{1,0:T(8,128)}, u32[]{:S(2)}) copy-start(f32[512,512]{1,0:T(8,128)} %get-tuple-element.58) | copy-start | bytes 3145732
  53.6 22.4 %collective-permute-start.2 = (f32[256,512]{1,0:T(8,128)S(1)}, f32[256,512]{1,0:T(8,128)S(1)}, u32[]{:S(2)}, u32[]{:S(2)}) collective-permute-start(f32[256,512]{1,0:T(8,128)S(1)} %get-tuple-element.99), channel_id=1, source_target_pairs={{0,2},{2,0},{1,3},{3,1},{4,6},{6,4},{5,7},{7,5}} | collective-permute-start | bytes 1572872 | tf_op jit(solution)/shard_map/ppermute | solution.py:519
  53.7 33.4 %collective-permute-start.3 = (f32[256,512]{1,0:T(8,128)S(1)}, f32[256,512]{1,0:T(8,128)S(1)}, u32[]{:S(2)}, u32[]{:S(2)}) collective-permute-start(f32[256,512]{1,0:T(8,128)S(1)} %get-tuple-element.98), channel_id=1, source_target_pairs={{0,2},{2,0},{1,3},{3,1},{4,6},{6,4},{5,7},{7,5}} | collective-permute-start | bytes 1572872 | tf_op jit(solution)/shard_map/ppermute | solution.py:519
  55.7 34.6 %collective-permute-start.15 = (bf16[512,512]{1,0:T(8,128)(2,1)}, bf16[512,512]{1,0:T(8,128)(2,1)S(1)}, u32[]{:S(2)}, u32[]{:S(2)}) collective-permute-start(bf16[512,512]{1,0:T(8,128)(2,1)} %refs_10_.3), channel_id=1, source_target_pairs={{0,1},{1,0},{2,3},{3,2},{4,5},{5,4},{6,7},{7,6}} | collective-permute-start | bytes 1572872 | tf_op jit(solution)/shard_map/ppermute | solution.py:519
  64.8 23.4 %copy-start.10 = (bf16[512,512]{1,0:T(8,128)(2,1)}, bf16[512,512]{1,0:T(8,128)(2,1)S(1)}, u32[]{:S(2)}) copy-start(bf16[512,512]{1,0:T(8,128)(2,1)S(1)} %collective-permute-done.13.refs_8_) | copy-start | bytes 1572868
  64.8 37.2 %collective-permute-start.14 = (bf16[512,512]{1,0:T(8,128)(2,1)S(1)}, bf16[512,512]{1,0:T(8,128)(2,1)S(1)}, u32[]{:S(2)}, u32[]{:S(2)}) collective-permute-start(bf16[512,512]{1,0:T(8,128)(2,1)S(1)} %collective-permute-done.13.refs_8_), channel_id=1, source_target_pairs={{0,1},{1,0},{2,3},{3,2},{4,5},{5,4},{6,7},{7,6}} | collective-permute-start | bytes 1572872 | tf_op jit(solution)/shard_map/ppermute | solution.py:519
  77.2 27.0 %copy-start.6 = (bf16[256,512]{1,0:T(8,128)(2,1)}, bf16[256,512]{1,0:T(8,128)(2,1)S(1)}, u32[]{:S(2)}) copy-start(bf16[256,512]{1,0:T(8,128)(2,1)S(1)} %fusion.5.refs_4_) | copy-start | bytes 786436
  88.2 9.2 %collective-permute-start.5 = (bf16[256,512]{1,0:T(8,128)(2,1)S(1)}, bf16[256,512]{1,0:T(8,128)(2,1)S(1)}, u32[]{:S(2)}, u32[]{:S(2)}) collective-permute-start(bf16[256,512]{1,0:T(8,128)(2,1)S(1)} %fusion.3.refs_5_), channel_id=1, source_target_pairs={{0,2},{2,0},{1,3},{3,1},{4,6},{6,4},{5,7},{7,5}} | collective-permute-start | bytes 786440 | tf_op jit(solution)/shard_map/ppermute | solution.py:519
  90.0 12.0 %collective-permute-start.4 = (bf16[256,512]{1,0:T(8,128)(2,1)S(1)}, bf16[256,512]{1,0:T(8,128)(2,1)S(1)}, u32[]{:S(2)}, u32[]{:S(2)}) collective-permute-start(bf16[256,512]{1,0:T(8,128)(2,1)S(1)} %fusion.5.refs_4_), channel_id=1, source_target_pairs={{0,2},{2,0},{1,3},{3,1},{4,6},{6,4},{5,7},{7,5}} | collective-permute-start | bytes 786440 | tf_op jit(solution)/shard_map/ppermute | solution.py:519
  90.2 11.7 %collective-permute-start.9 = (bf16[256,512]{1,0:T(8,128)(2,1)S(1)}, bf16[256,512]{1,0:T(8,128)(2,1)S(1)}, u32[]{:S(2)}, u32[]{:S(2)}) collective-permute-start(bf16[256,512]{1,0:T(8,128)(2,1)S(1)} %fusion.3.refs_5_), channel_id=1, source_target_pairs={{0,1},{1,0},{2,3},{3,2},{4,5},{5,4},{6,7},{7,6}} | collective-permute-start | bytes 786440 | tf_op jit(solution)/shard_map/ppermute | solution.py:519
  90.3 11.7 %collective-permute-start.8 = (bf16[256,512]{1,0:T(8,128)(2,1)S(1)}, bf16[256,512]{1,0:T(8,128)(2,1)S(1)}, u32[]{:S(2)}, u32[]{:S(2)}) collective-permute-start(bf16[256,512]{1,0:T(8,128)(2,1)S(1)} %fusion.5.refs_4_), channel_id=1, source_target_pairs={{0,1},{1,0},{2,3},{3,2},{4,5},{5,4},{6,7},{7,6}} | collective-permute-start | bytes 786440 | tf_op jit(solution)/shard_map/ppermute | solution.py:519
  97.4 4.6 %collective-permute-start.7 = (bf16[256,512]{1,0:T(8,128)(2,1)S(1)}, bf16[256,512]{1,0:T(8,128)(2,1)S(1)}, u32[]{:S(2)}, u32[]{:S(2)}) collective-permute-start(bf16[256,512]{1,0:T(8,128)(2,1)S(1)} %collective-permute-done.5.refs_1_), channel_id=1, source_target_pairs={{0,1},{1,0},{2,3},{3,2},{4,5},{5,4},{6,7},{7,6}} | collective-permute-start | bytes 786440 | tf_op jit(solution)/shard_map/ppermute | solution.py:519
  101.9 1.5 collective-permute-start.6
  128.3 2.9 collective-permute-start.17
  128.5 49.2 %collective-permute-start.16 = (f32[520,512]{1,0:T(8,128)}, f32[520,512]{1,0:T(8,128)}, u32[]{:S(2)}, u32[]{:S(2)}) collective-permute-start(f32[520,512]{1,0:T(8,128)} %get-tuple-element.79), channel_id=1, source_target_pairs={{0,1},{1,0},{2,3},{3,2},{4,5},{5,4},{6,7},{7,6}} | collective-permute-start | bytes 3194888 | tf_op jit(solution)/shard_map/ppermute | solution.py:519
  133.6 44.4 %collective-permute-start.18 = (f32[520,512]{1,0:T(8,128)}, f32[520,512]{1,0:T(8,128)}, u32[]{:S(2)}, u32[]{:S(2)}) collective-permute-start(f32[520,512]{1,0:T(8,128)} %add.73), channel_id=1, source_target_pairs={{0,2},{2,0},{1,3},{3,1},{4,6},{6,4},{5,7},{7,5}} | collective-permute-start | bytes 3194888 | tf_op jit(solution)/shard_map/ppermute | solution.py:519
  167.9 15.9 %collective-permute-start.11 = (f32[512,512]{1,0:T(8,128)}, f32[512,512]{1,0:T(8,128)S(1)}, u32[]{:S(2)}, u32[]{:S(2)}) collective-permute-start(f32[512,512]{1,0:T(8,128)} %get-tuple-element.76), channel_id=1, source_target_pairs={{0,1},{1,0},{2,3},{3,2},{4,5},{5,4},{6,7},{7,6}} | collective-permute-start | bytes 3145736 | tf_op jit(solution)/shard_map/ppermute | solution.py:519
  168.0 14.1 %collective-permute-start.21 = (bf16[512,512]{1,0:T(8,128)(2,1)}, bf16[512,512]{1,0:T(8,128)(2,1)S(1)}, u32[]{:S(2)}, u32[]{:S(2)}) collective-permute-start(bf16[512,512]{1,0:T(8,128)(2,1)} %refs_2_), channel_id=1, source_target_pairs={{0,1},{1,0},{2,3},{3,2},{4,5},{5,4},{6,7},{7,6}} | collective-permute-start | bytes 1572872 | tf_op jit(solution)/shard_map/ppermute | solution.py:519
  168.5 21.8 %collective-permute-start.20 = (bf16[512,512]{1,0:T(8,128)(2,1)}, bf16[512,512]{1,0:T(8,128)(2,1)S(1)}, u32[]{:S(2)}, u32[]{:S(2)}) collective-permute-start(bf16[512,512]{1,0:T(8,128)(2,1)} %refs_2_), channel_id=1, source_target_pairs={{0,3},{3,0},{1,2},{2,1},{4,7},{7,4},{5,6},{6,5}} | collective-permute-start | bytes 1572872 | tf_op jit(solution)/shard_map/ppermute | solution.py:519
  177.7 24.6 %collective-permute-start.19 = (bf16[512,512]{1,0:T(8,128)(2,1)}, bf16[512,512]{1,0:T(8,128)(2,1)S(1)}, u32[]{:S(2)}, u32[]{:S(2)}) collective-permute-start(bf16[512,512]{1,0:T(8,128)(2,1)} %refs_2_), channel_id=1, source_target_pairs={{0,2},{2,0},{1,3},{3,1},{4,6},{6,4},{5,7},{7,5}} | collective-permute-start | bytes 1572872 | tf_op jit(solution)/shard_map/ppermute | solution.py:519
  182.0 22.0 %collective-permute-start.24 = (bf16[512,512]{1,0:T(8,128)(2,1)S(1)}, bf16[512,512]{1,0:T(8,128)(2,1)S(1)}, u32[]{:S(2)}, u32[]{:S(2)}) collective-permute-start(bf16[512,512]{1,0:T(8,128)(2,1)S(1)} %fusion.1.refs_6_), channel_id=1, source_target_pairs={{0,1},{1,0},{2,3},{3,2},{4,5},{5,4},{6,7},{7,6}} | collective-permute-start | bytes 1572872 | tf_op jit(solution)/shard_map/ppermute | solution.py:519
  182.1 30.6 %collective-permute-start.23 = (bf16[512,512]{1,0:T(8,128)(2,1)S(1)}, bf16[512,512]{1,0:T(8,128)(2,1)S(1)}, u32[]{:S(2)}, u32[]{:S(2)}) collective-permute-start(bf16[512,512]{1,0:T(8,128)(2,1)S(1)} %fusion.1.refs_6_), channel_id=1, source_target_pairs={{0,3},{3,0},{1,2},{2,1},{4,7},{7,4},{5,6},{6,5}} | collective-permute-start | bytes 1572872 | tf_op jit(solution)/shard_map/ppermute | solution.py:519
  183.8 40.9 %collective-permute-start.22 = (bf16[512,512]{1,0:T(8,128)(2,1)S(1)}, bf16[512,512]{1,0:T(8,128)(2,1)S(1)}, u32[]{:S(2)}, u32[]{:S(2)}) collective-permute-start(bf16[512,512]{1,0:T(8,128)(2,1)S(1)} %fusion.1.refs_6_), channel_id=1, source_target_pairs={{0,2},{2,0},{1,3},{3,1},{4,6},{6,4},{5,7},{7,5}} | collective-permute-start | bytes 1572872 | tf_op jit(solution)/shard_map/ppermute | solution.py:519
  190.3 34.4 %copy-start.14 = (bf16[512,512]{1,0:T(8,128)(2,1)}, bf16[512,512]{1,0:T(8,128)(2,1)S(1)}, u32[]{:S(2)}) copy-start(bf16[512,512]{1,0:T(8,128)(2,1)S(1)} %collective-permute-done.20.refs_1_) | copy-start | bytes 1572868
  190.3 73.6 %collective-permute-start.10 = (f32[512,512]{1,0:T(8,128)}, f32[512,512]{1,0:T(8,128)}, u32[]{:S(2)}, u32[]{:S(2)}) collective-permute-start(f32[512,512]{1,0:T(8,128)} %get-tuple-element.74), channel_id=1, source_target_pairs={{0,1},{1,0},{2,3},{3,2},{4,5},{5,4},{6,7},{7,6}} | collective-permute-start | bytes 3145736 | tf_op jit(solution)/shard_map/ppermute | solution.py:519
  202.3 61.7 %collective-permute-start.12 = (f32[512,512]{1,0:T(8,128)}, f32[512,512]{1,0:T(8,128)}, u32[]{:S(2)}, u32[]{:S(2)}) collective-permute-start(f32[512,512]{1,0:T(8,128)} %add.69), channel_id=1, source_target_pairs={{0,2},{2,0},{1,3},{3,1},{4,6},{6,4},{5,7},{7,5}} | collective-permute-start | bytes 3145736 | tf_op jit(solution)/shard_map/ppermute | solution.py:519
  249.7 17.9 %collective-permute-start.26 = (f32[520,512]{1,0:T(8,128)}, f32[520,512]{1,0:T(8,128)}, u32[]{:S(2)}, u32[]{:S(2)}) collective-permute-start(f32[520,512]{1,0:T(8,128)} %get-tuple-element.89), channel_id=1, source_target_pairs={{0,1},{1,0},{2,3},{3,2},{4,5},{5,4},{6,7},{7,6}} | collective-permute-start | bytes 3194888 | tf_op jit(solution)/shard_map/ppermute | solution.py:519
  267.2 47.5 %collective-permute-start.25 = (f32[520,512]{1,0:T(8,128)}, f32[520,512]{1,0:T(8,128)}, u32[]{:S(2)}, u32[]{:S(2)}) collective-permute-start(f32[520,512]{1,0:T(8,128)} %get-tuple-element.87), channel_id=1, source_target_pairs={{0,1},{1,0},{2,3},{3,2},{4,5},{5,4},{6,7},{7,6}} | collective-permute-start | bytes 3194888 | tf_op jit(solution)/shard_map/ppermute | solution.py:519
  270.1 53.7 %collective-permute-start.27 = (f32[520,512]{1,0:T(8,128)}, f32[520,512]{1,0:T(8,128)}, u32[]{:S(2)}, u32[]{:S(2)}) collective-permute-start(f32[520,512]{1,0:T(8,128)} %add.77), channel_id=1, source_target_pairs={{0,2},{2,0},{1,3},{3,1},{4,6},{6,4},{5,7},{7,5}} | collective-permute-start | bytes 3194888 | tf_op jit(solution)/shard_map/ppermute | solution.py:519
  (21 other events, 147.4 us)
